TPU v7x, 8 devices: a whole 2x2x1 slice. The times are simulated.
8 devices in a mesh: rep: 1 (over z), dp: 8 (over x, y, core).
Axes of the slice: x: 2, y: 2, z: 1, core: 2. Of those that a mesh axis runs over, the one named last changes fastest.
Arguments:
- x: bfloat16 [8, 2048, 640], P(('rep', 'dp'))
- dy: bfloat16 [8, 2048, 640], P(('rep', 'dp'))
- w_gate: bfloat16 [2, 640, 4096], P(None, 'dp')
- w_up: bfloat16 [2, 640, 4096], P(None, 'dp')
- w_down: bfloat16 [2, 4096, 640], P(None, 'dp')
Outputs:
- output 1: bfloat16 [8, 2048, 640], P(('rep', 'dp'))
- output 2: bfloat16 [2, 640, 4096], P('rep', 'dp')
- output 3: bfloat16 [2, 640, 4096], P('rep', 'dp')
- output 4: bfloat16 [2, 4096, 640], P('rep', 'dp')
All inputs are finite; a program needn't handle non-finite values.
Results may differ from a plain program's by a relative error of at most 0.018.
Values are sent between devices in bfloat16 or wider.
A program may use at most 2 GiB of HBM per device.

v0:
```python
import jax
import jax.numpy as jnp
from jax import lax

NAMES = ("w_gate", "w_up", "w_down")


def matmul(a, w):
    return jnp.dot(a, w, preferred_element_type=jnp.float32).astype(jnp.bfloat16)


def normed(h):
    wide = h.astype(jnp.float32)
    scale = lax.rsqrt(jnp.mean(wide**2, -1, keepdims=True) + 1e-6)
    return (wide * scale).astype(jnp.bfloat16)


def layer(h, w):
    a = normed(h)
    gate = jnp.dot(a, w["w_gate"], preferred_element_type=jnp.float32)
    up = jnp.dot(a, w["w_up"], preferred_element_type=jnp.float32)
    return h + matmul((jax.nn.silu(gate) * up).astype(jnp.bfloat16), w["w_down"])


def stack(weights, h):
    for number in range(weights["w_gate"].shape[0]):
        h = layer(h, {name: w[number] for name, w in weights.items()})
    return h


def solution(mesh):
    groups = mesh.shape["rep"]

    def step(x, dy, *weights):
        shape = x.shape
        x, dy = (t.reshape(groups, -1, *t.shape[1:]) for t in (x, dy))

        def of_a_group(x, dy):
            _, back = jax.vjp(stack, dict(zip(NAMES, weights, strict=True)), x)
            by_weights, by_x = back(dy)
            return (by_x, *(by_weights[name] for name in NAMES))

        by_x, *by_weights = jax.vmap(of_a_group)(x, dy)
        return (by_x.reshape(shape), *(t.reshape(-1, *t.shape[2:]) for t in by_weights))

    return step
```

profile of v0, /device:TPU:0, one launch (start us, length us, event | category | flops | bytes accessed | tf_op | source)
XLA Modules:
  0.0 814.1 jit_solution(13061735860020196922)
XLA Ops:
  24.2 23.7 %all-gather.30.cloned.1.call-done = bf16[1,640,4096]{2,1,0:T(8,128)(2,1)} async-done(((bf16[1,80,4096]{2,1,0:T(8,128)(2,1)}), bf16[1,640,4096]{2,1,0:T(8,128)(2,1)}) %all-gather.30.cloned.1.call-update) | async-done | bytes 5242896 | tf_op jit(solution)/vmap(jvp())/squeeze | solution.py:27
  47.9 19.7 %fusion.58 = f32[2048,4096]{1,0:T(8,128)} fusion(bf16[1,640,4096]{2,1,0:T(8,128)(2,1)} %all-gather.30.cloned.1.call-done, bf16[1,2048,640]{1,2,0:T(8,128)(2,1)S(1)} %copy.1, f32[2048]{0:T(1024)S(1)} %bitcast.307), kind=kOutput, calls=%fused_computation.79 | convolution fusion | flops 10741350400 | bytes 41426944 | tf_op jit(solution)/vmap(jvp())/dot_general | solution.py:20
  67.7 17.8 %all-gather.32.cloned.1.call-done = bf16[1,640,4096]{2,1,0:T(8,128)(2,1)} async-done(((bf16[1,80,4096]{2,1,0:T(8,128)(2,1)}), bf16[1,640,4096]{2,1,0:T(8,128)(2,1)}) %all-gather.32.cloned.1.call-update) | async-done | bytes 5242896 | tf_op jit(solution)/vmap(jvp())/squeeze | solution.py:27
  85.5 19.7 %fusion.54 = f32[2048,4096]{1,0:T(8,128)} fusion(bf16[1,640,4096]{2,1,0:T(8,128)(2,1)} %all-gather.32.cloned.1.call-done, bf16[1,2048,640]{1,2,0:T(8,128)(2,1)S(1)} %copy.1, f32[2048]{0:T(1024)S(1)} %bitcast.308), kind=kOutput, calls=%fused_computation.75 | convolution fusion | flops 10741350400 | bytes 41426944 | tf_op jit(solution)/vmap(jvp())/dot_general | solution.py:21
  105.2 27.5 %fusion.24 = bf16[2048,4096]{1,0:T(8,128)(2,1)} fusion(f32[2048,4096]{1,0:T(8,128)} %fusion.54, f32[2048,4096]{1,0:T(8,128)} %fusion.58), kind=kLoop, calls=%fused_computation.34 | loop fusion | flops 50331648 | bytes 83886080
  132.7 17.9 %fusion.39 = (f32[2048]{0:T(1024)S(1)}, bf16[1,2048,640]{1,2,0:T(8,128)(2,1)}) fusion(bf16[1,2048,640]{1,2,0:T(8,128)(2,1)S(1)} %copy.1, bf16[2048,4096]{1,0:T(8,128)(2,1)} %fusion.24, bf16[1,4096,640]{2,1,0:T(8,128)(2,1)} %all-gather.34.cloned.1.call-done), kind=kOutput, calls=%fused_computation.60 | convolution fusion | flops 10743969792 | bytes 27271168 | tf_op jit(solution)/vmap(jvp())/dot_general | solution.py:9
  159.9 22.3 %fusion.42 = f32[2048,4096]{1,0:T(8,128)} fusion(bf16[1,640,4096]{2,1,0:T(8,128)(2,1)} %all-gather.40.cloned.1.call-done, bf16[1,2048,640]{1,2,0:T(8,128)(2,1)} %get-tuple-element.11, f32[2048]{0:T(1024)S(1)} %bitcast.312), kind=kOutput, calls=%fused_computation.63 | convolution fusion | flops 10741350400 | bytes 41426944 | tf_op jit(solution)/vmap(jvp())/dot_general | solution.py:21
  197.3 19.8 %fusion.48 = f32[2048,4096]{1,0:T(8,128)} fusion(bf16[1,640,4096]{2,1,0:T(8,128)(2,1)} %all-gather.36.cloned.1.call-done, bf16[1,2048,640]{1,2,0:T(8,128)(2,1)S(1)} %copy-done.6, f32[2048]{0:T(1024)S(1)} %bitcast.313), kind=kOutput, calls=%fused_computation.69 | convolution fusion | flops 10741350400 | bytes 41426944 | tf_op jit(solution)/vmap(jvp())/dot_general | solution.py:20
  217.1 17.0 %all-gather.38.cloned.1.call-done = bf16[1,4096,640]{2,1,0:T(8,128)(2,1)} async-done(((bf16[1,512,640]{2,1,0:T(8,128)(2,1)}), bf16[1,4096,640]{2,1,0:T(8,128)(2,1)}) %all-gather.38.cloned.1.call-update) | async-done | bytes 5242896 | tf_op jit(solution)/vmap(jvp())/squeeze | solution.py:27
  234.2 27.4 %convolution_convert_fusion.1 = bf16[2048,4096]{1,0:T(8,128)(2,1)} fusion(bf16[1,4096,640]{2,1,0:T(8,128)(2,1)} %all-gather.38.cloned.1.call-done, bf16[1,2048,640]{2,1,0:T(8,128)(2,1)} %param), kind=kOutput, calls=%fused_computation.42 | convolution fusion | flops 10745806848 | bytes 24641536 | tf_op jit(solution)/vmap(transpose(jvp()))/dot_general | solution.py:9
  261.5 27.1 %fusion.4 = bf16[2048,4096]{1,0:T(8,128)(2,1)S(1)} fusion(f32[2048,4096]{1,0:T(8,128)} %fusion.48, f32[2048,4096]{1,0:T(8,128)} %fusion.42, bf16[2048,4096]{1,0:T(8,128)(2,1)} %convolution_convert_fusion.1), kind=kLoop, calls=%fused_computation.10 | loop fusion | flops 100663296 | bytes 100663296
  307.8 22.4 %fusion.41 = (f32[2048]{0:T(1024)S(1)}, bf16[1,2048,640]{1,2,0:T(8,128)(2,1)S(1)}) fusion(bf16[1,2048,640]{1,2,0:T(8,128)(2,1)S(1)} %copy-done.6, bf16[2048,640]{0,1:T(8,128)(2,1)S(1)} %fusion.63, bf16[1,640,4096]{2,1,0:T(8,128)(2,1)} %all-gather.40.cloned.1.call-done, bf16[2048,4096]{1,0:T(8,128)(2,1)} %convolution_convert_fusion.1, f32[2048,4096]{1,0:T(8,128)} %fusion.48), kind=kOutput, calls=%fused_computation.62 | convolution fusion | flops 10795612160 | bytes 63447040 | tf_op jit(solution)/vmap(transpose(jvp()))/dot_general | solution.py:21
  333.6 18.8 %fusion.109 = f32[640,4096]{0,1:T(8,128)} fusion(bf16[2048,4096]{1,0:T(8,128)(2,1)} %fusion.24, bf16[1,2048,640]{1,2,0:T(8,128)(2,1)S(1)} %fusion.108), kind=kOutput, calls=%fused_computation.96 | convolution fusion | flops 10737418240 | bytes 29884416 | tf_op jit(solution)/vmap(transpose(jvp()))/dot_general | solution.py:9
  352.5 31.2 %fusion.26 = f32[4096,640]{1,0:T(8,128)} fusion(f32[2048,4096]{1,0:T(8,128)} %fusion.42, f32[2048,4096]{1,0:T(8,128)} %fusion.48, bf16[1,2048,640]{2,1,0:T(8,128)(2,1)} %param), kind=kOutput, calls=%fused_computation.36 | convolution fusion | flops 10787749888 | bytes 80216064 | tf_op jit(solution)/vmap(transpose(jvp()))/dot_general | solution.py:9
  383.7 25.0 %fusion.20 = f32[4096,640]{0,1:T(8,128)} fusion(bf16[2048,4096]{1,0:T(8,128)(2,1)} %convolution_convert_fusion.1, f32[2048,4096]{1,0:T(8,128)} %fusion.48, bf16[1,2048,640]{1,2,0:T(8,128)(2,1)S(1)} %copy-done.6, f32[2048]{0:T(1024)S(1)} %bitcast.315), kind=kOutput, calls=%fused_computation.32 | convolution fusion | flops 10791682048 | bytes 63447040 | tf_op jit(solution)/vmap(transpose(jvp()))/dot_general | solution.py:21
  408.8 20.0 %convolution_convert_fusion = bf16[2048,4096]{1,0:T(8,128)(2,1)} fusion(bf16[1,4096,640]{2,1,0:T(8,128)(2,1)} %all-gather.34.cloned.1.call-done, bf16[1,2048,640]{1,2,0:T(8,128)(2,1)} %copy-done.3), kind=kOutput, calls=%fused_computation.41 | convolution fusion | flops 10745806848 | bytes 24641536 | tf_op jit(solution)/vmap(transpose(jvp()))/dot_general | solution.py:9
  428.8 24.9 %fusion.16 = f32[4096,640]{0,1:T(8,128)} fusion(bf16[2048,4096]{1,0:T(8,128)(2,1)} %convolution_convert_fusion, f32[2048,4096]{1,0:T(8,128)} %fusion.58, bf16[1,2048,640]{1,2,0:T(8,128)(2,1)S(1)} %copy-done.1, f32[2048]{0:T(1024)S(1)} %bitcast.309), kind=kOutput, calls=%fused_computation.30 | convolution fusion | flops 10791682048 | bytes 63447040 | tf_op jit(solution)/vmap(transpose(jvp()))/dot_general | solution.py:21
  453.8 17.7 %fusion.120 = f32[4096,640]{0,1:T(8,128)} fusion(bf16[2048,4096]{1,0:T(8,128)(2,1)} %copy-done.2, bf16[1,2048,640]{1,2,0:T(8,128)(2,1)} %get-tuple-element.11, f32[2048]{0:T(1024)S(1)} %bitcast.316), kind=kOutput, calls=%fused_computation.102 | convolution fusion | flops 10741350400 | bytes 29892608 | tf_op jit(solution)/vmap(transpose(jvp()))/dot_general | solution.py:20
  471.6 33.1 %fusion.7 = bf16[2048,4096]{1,0:T(8,128)(2,1)} fusion(f32[2048,4096]{1,0:T(8,128)} %fusion.58, f32[2048,4096]{1,0:T(8,128)} %fusion.54, bf16[2048,4096]{1,0:T(8,128)(2,1)} %convolution_convert_fusion), kind=kLoop, calls=%fused_computation.13 | loop fusion | flops 100663296 | bytes 100663296
  504.8 17.0 %fusion.115 = f32[4096,640]{0,1:T(8,128)} fusion(bf16[2048,4096]{1,0:T(8,128)(2,1)} %fusion.7, bf16[1,2048,640]{1,2,0:T(8,128)(2,1)S(1)} %copy-done.1, f32[2048]{0:T(1024)S(1)} %bitcast.310), kind=kOutput, calls=%fused_computation.101 | convolution fusion | flops 10741350400 | bytes 29892608 | tf_op jit(solution)/vmap(transpose(jvp()))/dot_general | solution.py:20
  537.9 22.4 %fusion.38 = (f32[2048]{0:T(1024)S(1)}, bf16[1,2048,640]{1,2,0:T(8,128)(2,1)S(1)}) fusion(bf16[1,2048,640]{1,2,0:T(8,128)(2,1)S(1)} %copy-done.1, bf16[2048,640]{0,1:T(8,128)(2,1)S(1)} %fusion.60, bf16[1,640,4096]{2,1,0:T(8,128)(2,1)} %all-gather.32.cloned.1.call-done, bf16[2048,4096]{1,0:T(8,128)(2,1)} %convolution_convert_fusion, f32[2048,4096]{1,0:T(8,128)} %fusion.58), kind=kOutput, calls=%fused_computation.59 | convolution fusion | flops 10795612160 | bytes 63447040 | tf_op jit(solution)/vmap(transpose(jvp()))/dot_general | solution.py:21
  578.2 74.4 %reduce-scatter.25.cloned.1.call-done = f32[4096,80]{0,1:T(8,128)} async-done(((f32[4096,640]{0,1:T(8,128)}), f32[4096,80]{0,1:T(8,128)}) %reduce-scatter.25.cloned.1.call-update) | async-done | bytes 1310736
  655.1 73.4 %reduce-scatter.19.cloned.1.call-done = f32[4096,80]{0,1:T(8,128)} async-done(((f32[4096,640]{0,1:T(8,128)}), f32[4096,80]{0,1:T(8,128)}) %reduce-scatter.19.cloned.1.call-update) | async-done | bytes 1310736
  729.9 74.4 %reduce-scatter.21.cloned.1.call-done = f32[4096,80]{0,1:T(8,128)} async-done(((f32[4096,640]{0,1:T(8,128)}), f32[4096,80]{0,1:T(8,128)}) %reduce-scatter.21.cloned.1.call-update) | async-done | bytes 1310736
  (84 shorter events, 104.6 us)
Async XLA Ops:
  7.2 5.2 copy-start.7
  7.2 40.8 %all-gather.30.cloned.1.call-start = ((), (), s32[]{:S(2)}) async-start(), calls=%async_computation.6 | async-start | bytes 5898240 | tf_op jit(solution)/vmap(jvp())/squeeze | solution.py:27
  9.8 75.7 %all-gather.32.cloned.1.call-start = ((), (), s32[]{:S(2)}) async-start(), calls=%async_computation.7 | async-start | bytes 5898240 | tf_op jit(solution)/vmap(jvp())/squeeze | solution.py:27
  12.3 120.4 %all-gather.34.cloned.1.call-start = ((), (), s32[]{:S(2)}) async-start(), calls=%async_computation.8 | async-start | bytes 5898240 | tf_op jit(solution)/vmap(jvp())/squeeze | solution.py:27
  13.6 146.3 %all-gather.40.cloned.1.call-start = ((), (), s32[]{:S(2)}) async-start(), calls=%async_computation.11 | async-start | bytes 5898240 | tf_op jit(solution)/vmap(jvp())/squeeze | solution.py:27
  14.2 183.1 %all-gather.36.cloned.1.call-start = ((), (), s32[]{:S(2)}) async-start(), calls=%async_computation.9 | async-start | bytes 5898240 | tf_op jit(solution)/vmap(jvp())/squeeze | solution.py:27
  14.8 219.4 %all-gather.38.cloned.1.call-start = ((), (), s32[]{:S(2)}) async-start(), calls=%async_computation.10 | async-start | bytes 5898240 | tf_op jit(solution)/vmap(jvp())/squeeze | solution.py:27
  15.3 552.8 %reduce-scatter.29.cloned.1.call-start = ((), (), s32[]{:S(2)}) async-start(), calls=%async_computation.17 | async-start | bytes 11796480
  18.4 114.4 %copy-start = (bf16[1,2048,640]{1,2,0:T(8,128)(2,1)}, bf16[1,2048,640]{1,2,0:T(8,128)(2,1)S(1)}, u32[]{:S(2)}) copy-start(bf16[1,2048,640]{1,2,0:T(8,128)(2,1)S(1)} %copy.1) | copy-start | bytes 7864324
  19.8 65.7 %copy-start.12 = (f32[1,2048]{1,0:T(1,128)}, f32[1,2048]{1,0:T(1,128)S(1)}, u32[]{:S(2)}) copy-start(f32[1,2048]{1,0:T(1,128)S(1)} %rsqrt.22) | copy-start | bytes 24580
  159.9 37.4 %copy-start.6 = (bf16[1,2048,640]{1,2,0:T(8,128)(2,1)S(1)}, bf16[1,2048,640]{1,2,0:T(8,128)(2,1)}, u32[]{:S(2)}) copy-start(bf16[1,2048,640]{1,2,0:T(8,128)(2,1)} %get-tuple-element.11) | copy-start | bytes 7864324
  288.6 5.7 copy-start.2
  307.8 22.4 %copy-start.11 = (f32[2048]{0:T(1024)S(1)}, f32[2048]{0:T(1024)}, u32[]{:S(2)}) copy-start(f32[2048]{0:T(1024)} %copy-done.10) | copy-start | bytes 24580
  307.8 22.5 %copy-start.5 = (bf16[1,2048,640]{1,2,0:T(8,128)(2,1)S(1)}, bf16[1,2048,640]{1,2,0:T(8,128)(2,1)}, u32[]{:S(2)}) copy-start(bf16[1,2048,640]{1,2,0:T(8,128)(2,1)} %copy.2) | copy-start | bytes 7864324
  332.1 1.5 copy-start.3
  352.5 217.1 %reduce-scatter.27.cloned.1.call-start = ((), (), s32[]{:S(2)}) async-start(), calls=%async_computation.16 | async-start | bytes 11796480
  383.7 193.1 %reduce-scatter.23.cloned.1.call-start = ((), (), s32[]{:S(2)}) async-start(), calls=%async_computation.14 | async-start | bytes 11796480
  408.8 20.0 %copy-start.1 = (bf16[1,2048,640]{1,2,0:T(8,128)(2,1)S(1)}, bf16[1,2048,640]{1,2,0:T(8,128)(2,1)}, u32[]{:S(2)}) copy-start(bf16[1,2048,640]{1,2,0:T(8,128)(2,1)} %copy-done) | copy-start | bytes 7864324
  408.8 20.0 %copy-start.13 = (f32[1,2048]{1,0:T(1,128)S(1)}, f32[1,2048]{1,0:T(1,128)}, u32[]{:S(2)}) copy-start(f32[1,2048]{1,0:T(1,128)} %copy-done.12) | copy-start | bytes 24580
  408.8 243.8 %reduce-scatter.25.cloned.1.call-start = ((), (), s32[]{:S(2)}) async-start(), calls=%async_computation.15 | async-start | bytes 11796480
  453.8 274.7 %reduce-scatter.19.cloned.1.call-start = ((), (), s32[]{:S(2)}) async-start(), calls=%async_computation.12 | async-start | bytes 11796480
  471.6 332.7 %reduce-scatter.21.cloned.1.call-start = ((), (), s32[]{:S(2)}) async-start(), calls=%async_computation.13 | async-start | bytes 11796480
  537.9 22.4 %copy-start.9 = (f32[2048]{0:T(1024)S(1)}, f32[2048]{0:T(1024)}, u32[]{:S(2)}) copy-start(f32[2048]{0:T(1024)} %copy-done.8) | copy-start | bytes 24580
  537.9 22.5 %copy-start.4 = (bf16[1,2048,640]{1,2,0:T(8,128)(2,1)S(1)}, bf16[1,2048,640]{1,2,0:T(8,128)(2,1)}, u32[]{:S(2)}) copy-start(bf16[1,2048,640]{1,2,0:T(8,128)(2,1)} %copy-done.3) | copy-start | bytes 7864324
  (2 other events, 1.4 us)
Sparse Core Ops, SparseCore 0:
  9.9 37.9 all-gather.29
  50.3 35.1 all-gather.31
  87.3 35.1 all-gather.33
  124.7 35.1 all-gather.39
  162.1 35.1 all-gather.35
  199.0 35.1 all-gather.37
  352.6 72.4 reduce-scatter.28
  428.5 72.4 reduce-scatter.26
  504.4 72.4 reduce-scatter.22
  580.1 72.4 reduce-scatter.24
  656.0 72.4 reduce-scatter.18
  731.8 72.4 reduce-scatter.20
where the time goes:
time: 822 us; the launch traced here: 814 us
  matrix products  356 us (43%)
  waiting for transfers between devices  311 us (38%)
  other arithmetic  105 us (13%)
  local copies, waits for them, and re-layouts  26.7 us (3%)
  between operations  14.9 us (2%)
    unnamed x18, waiting for transfers between devices  229 us
    dot_general x6, matrix products, layer(): up = jnp.dot(a, w['w_up'], preferred_element_type=jnp.float32)  137 us
    dot_general x5, matrix products, matmul(): jnp.dot(a, w, preferred_element_type=jnp.float32).astype(jnp.bfloat16)  115 us
    dot_general x6, matrix products, layer(): gate = jnp.dot(a, w['w_gate'], preferred_element_type=jnp.float32)  104 us
    unnamed x3, other arithmetic  87.7 us
    squeeze x6, waiting for transfers between devices, stack(): h = layer(h, {name: w[number] for name, w in weights.items()})  82.4 us
    unnamed x31, local copies, waits for them, and re-layouts  20.4 us
  transfers between devices with their start and end apart: 12, of which 9 were waited for; matrix products, arithmetic and copies ran while one was open for 45% of the time, Pallas kernels for 0%

commit v1 on v0

v1 whole, which is shorter than its diff:
```python
import jax
import jax.numpy as jnp
from jax import lax
from jax.experimental import pallas as pl
from jax.experimental.pallas import tpu as pltpu
from jax.sharding import PartitionSpec as P

N = 8
T, D, FF, LAYERS = 2048, 640, 4096, 2
CH = 4
F = FF // CH
RB = D // N
CB = F // N
HD = D // 2
STEPS = LAYERS * CH
TB = 512
VB = 256

f32, bf16 = jnp.float32, jnp.bfloat16


def dot(a, b):
    return jnp.dot(a, b, preferred_element_type=f32)


def dot_nt(a, b):
    return lax.dot_general(a, b, (((1,), (1,)), ((), ())), preferred_element_type=f32)


def kernel(
    x_hbm, dy_hbm, gu_own, dn_own,
    dx_hbm, outg_hbm, outd_hbm, gu_all, dn_all,
    wg, wu, wd, h, a, at, dy, dyt, z, dg, du, acc,
    owng, ownd, sibg, sibd, recg, recd, sdg, sdd, rdg, rdd,
    sxg, sxd, syg, syd, bxg, bxd, byg, byd, fing, find, og, od,
    ag_send, ag_recv, load_sem, rs_send, rs_recv, out_sem, in_sem, free_sib, free_diag, free_block,
):
    me = lax.axis_index("dp")
    k = me % 2
    cy = (me // 2) % 2
    cx = me // 4
    chip = 2 * cx + cy
    sib = 2 * chip + (1 - k)
    chip_x = 2 * (1 - cx) + cy
    chip_y = 2 * cx + (1 - cy)
    chip_d = 2 * (1 - cx) + (1 - cy)
    xn, yn, dn = 2 * chip_x + k, 2 * chip_y + k, 2 * chip_d + k

    def far(src, dst, ss, rs, to):
        return pltpu.make_async_remote_copy(
            src_ref=src, dst_ref=dst, send_sem=ss, recv_sem=rs, device_id={"dp": to}, device_id_type=pl.DeviceIdType.MESH
        )

    def signal(sem, to):
        pl.semaphore_signal(sem, inc=1, device_id={"dp": to}, device_id_type=pl.DeviceIdType.MESH)

    def own_copies(j):
        for i, to in enumerate((xn, yn, sib)):
            r = (0, 2, 8)[i]
            yield far(gu_own.at[j], gu_all.at[j, me], ag_send.at[2 * i], ag_recv.at[j, r], to)
            yield far(dn_own.at[j], dn_all.at[j, me], ag_send.at[2 * i + 1], ag_recv.at[j, r + 1], to)

    def forward_copies(j):
        top, bot = pl.ds(0, HD), pl.ds(HD, HD)
        yield far(gu_all.at[j, xn, 0], gu_all.at[j, xn, 0], ag_send.at[6], ag_recv.at[j, 4], yn)
        yield far(dn_all.at[j, xn, top], dn_all.at[j, xn, top], ag_send.at[7], ag_recv.at[j, 5], yn)
        yield far(gu_all.at[j, yn, 1], gu_all.at[j, yn, 1], ag_send.at[8], ag_recv.at[j, 6], xn)
        yield far(dn_all.at[j, yn, bot], dn_all.at[j, yn, bot], ag_send.at[9], ag_recv.at[j, 7], xn)
        for i, src in enumerate((xn, yn)):
            yield far(gu_all.at[j, src], gu_all.at[j, src], ag_send.at[10 + 2 * i], ag_recv.at[j, 10 + 2 * i], sib)
            yield far(dn_all.at[j, src], dn_all.at[j, src], ag_send.at[11 + 2 * i], ag_recv.at[j, 11 + 2 * i], sib)

    def last_copies(j):
        yield far(gu_all.at[j, dn], gu_all.at[j, dn], ag_send.at[14], ag_recv.at[j, 14], sib)
        yield far(dn_all.at[j, dn], dn_all.at[j, dn], ag_send.at[15], ag_recv.at[j, 15], sib)

    def arrived(ref, j, r, frm):
        far(ref, ref, ag_send.at[0], ag_recv.at[j, r], frm).wait_recv()

    def gather_own(j):
        @pl.when(j > 0)
        def _():
            for copy in own_copies(j):
                copy.wait_send()

        for copy in own_copies(j):
            copy.start()

    def gather_forward(j):
        arrived(gu_all.at[j, xn], j, 0, xn)
        arrived(dn_all.at[j, xn], j, 1, xn)
        arrived(gu_all.at[j, yn], j, 2, yn)
        arrived(dn_all.at[j, yn], j, 3, yn)

        @pl.when(j > 0)
        def _():
            for copy in forward_copies(j):
                copy.wait_send()

        for copy in forward_copies(j):
            copy.start()

    def gather_last(j):
        top, bot = pl.ds(0, HD), pl.ds(HD, HD)
        arrived(gu_all.at[j, dn, 0], j, 4, yn)
        arrived(dn_all.at[j, dn, top], j, 5, yn)
        arrived(gu_all.at[j, dn, 1], j, 6, xn)
        arrived(dn_all.at[j, dn, bot], j, 7, xn)

        @pl.when(j > 0)
        def _():
            for copy in last_copies(j):
                copy.wait_send()

        for copy in last_copies(j):
            copy.start()

    def gather_done(j):
        for i, c in enumerate((chip, chip_x, chip_y, chip_d)):
            src = 2 * c + (1 - k)
            r = 8 + 2 * i
            arrived(gu_all.at[j, src], j, r, sib)
            arrived(dn_all.at[j, src], j, r + 1, sib)

    def load_weights(j, slot):
        def parts(gu, down, src):
            rows = pl.ds(pl.multiple_of(src * RB, RB), RB)
            cols = pl.ds(pl.multiple_of(src * CB, CB), CB)
            pltpu.make_async_copy(gu.at[0], wg.at[slot, rows], load_sem.at[slot, 0]).start()
            pltpu.make_async_copy(gu.at[1], wu.at[slot, rows], load_sem.at[slot, 1]).start()
            pltpu.make_async_copy(down, wd.at[slot, :, cols], load_sem.at[slot, 2]).start()

        parts(gu_own.at[j], dn_own.at[j], me)
        for i in range(1, N):
            src = (me + i) % N
            parts(gu_all.at[j, src], dn_all.at[j, src], src)

    def weights_loaded(slot):
        for i, w in enumerate((wg, wu, wd)):
            pltpu.make_async_copy(w.at[slot], w.at[slot], load_sem.at[slot, i]).wait()

    def sib_copies():
        return (
            far(sibg, recg, rs_send.at[0], rs_recv.at[0], sib),
            far(sibd, recd, rs_send.at[1], rs_recv.at[1], sib),
        )

    def diag_copies():
        top, bot = pl.ds(0, HD), pl.ds(HD, HD)
        return (
            far(sdg.at[0], rdg.at[0], rs_send.at[2], rs_recv.at[2], xn),
            far(sdd.at[top], rdd.at[top], rs_send.at[3], rs_recv.at[3], xn),
            far(sdg.at[1], rdg.at[1], rs_send.at[4], rs_recv.at[4], yn),
            far(sdd.at[bot], rdd.at[bot], rs_send.at[5], rs_recv.at[5], yn),
        )

    def block_copies():
        return (
            far(sxg, bxg, rs_send.at[6], rs_recv.at[6], xn),
            far(sxd, bxd, rs_send.at[7], rs_recv.at[7], xn),
            far(syg, byg, rs_send.at[8], rs_recv.at[8], yn),
            far(syd, byd, rs_send.at[9], rs_recv.at[9], yn),
        )

    def out_copies(j):
        return (
            pltpu.make_async_copy(og, outg_hbm.at[j], out_sem.at[0]),
            pltpu.make_async_copy(od, outd_hbm.at[j], out_sem.at[1]),
        )

    def scatter_sib(s):
        @pl.when(s > 0)
        def _():
            pl.semaphore_wait(free_sib, 1)

        for copy in sib_copies():
            copy.start()

    def scatter_diag(s):
        @pl.when(s > 0)
        def _():
            for copy in diag_copies():
                copy.wait_send()

        for copy in sib_copies():
            copy.wait_recv()
        for m in range(2):
            fing[m] = owng[m, chip] + recg[m, chip].astype(f32)
            owng[m, chip_x] = owng[m, chip_x] + recg[m, chip_x].astype(f32)
            owng[m, chip_y] = owng[m, chip_y] + recg[m, chip_y].astype(f32)
            sdg[m] = (owng[m, chip_d] + recg[m, chip_d].astype(f32)).astype(bf16)
        find[...] = ownd[chip] + recd[chip].astype(f32)
        ownd[chip_x] = ownd[chip_x] + recd[chip_x].astype(f32)
        ownd[chip_y] = ownd[chip_y] + recd[chip_y].astype(f32)
        sdd[...] = (ownd[chip_d] + recd[chip_d].astype(f32)).astype(bf16)

        @pl.when(s < STEPS - 1)
        def _():
            signal(free_sib, sib)

        @pl.when(s > 0)
        def _():
            for sem in (free_diag.at[0], free_diag.at[1]):
                pl.semaphore_wait(sem, 1)

        for copy in diag_copies():
            copy.start()

    def scatter_block(s):
        @pl.when(s > 0)
        def _():
            for copy in block_copies():
                copy.wait_send()

        for copy in diag_copies():
            copy.wait_recv()
        top, bot = pl.ds(0, HD), pl.ds(HD, HD)
        sxg[0] = owng[0, chip_x].astype(bf16)
        sxg[1] = (owng[1, chip_x] + rdg[1].astype(f32)).astype(bf16)
        sxd[top] = ownd[chip_x, top].astype(bf16)
        sxd[bot] = (ownd[chip_x, bot] + rdd[bot].astype(f32)).astype(bf16)
        syg[0] = (owng[0, chip_y] + rdg[0].astype(f32)).astype(bf16)
        syg[1] = owng[1, chip_y].astype(bf16)
        syd[top] = (ownd[chip_y, top] + rdd[top].astype(f32)).astype(bf16)
        syd[bot] = ownd[chip_y, bot].astype(bf16)

        @pl.when(s < STEPS - 1)
        def _():
            signal(free_diag.at[0], xn)
            signal(free_diag.at[1], yn)

        @pl.when(s > 0)
        def _():
            for sem in (free_block.at[0], free_block.at[1]):
                pl.semaphore_wait(sem, 1)

        for copy in block_copies():
            copy.start()

    def scatter_final(s):
        j = CH * (1 - s // CH) + s % CH

        @pl.when(s > 0)
        def _():
            for copy in out_copies(j):
                copy.wait()

        for copy in block_copies():
            copy.wait_recv()
        for m in range(2):
            og[m] = (fing[m] + bxg[m].astype(f32) + byg[m].astype(f32)).astype(bf16)
        od[...] = (find[...] + bxd[...].astype(f32) + byd[...].astype(f32)).astype(bf16)

        @pl.when(s < STEPS - 1)
        def _():
            signal(free_block.at[0], xn)
            signal(free_block.at[1], yn)

        for copy in out_copies(j):
            copy.start()

    def scale_of(wide):
        return lax.rsqrt(jnp.mean(wide * wide, -1, keepdims=True) + 1e-6)

    def tokens(t, n):
        return pl.ds(pl.multiple_of(t * n, n), n)

    def set_a(rows, wide):
        v = (wide * scale_of(wide)).astype(bf16)
        a[rows, :] = v
        vt = v.T
        for d in range(N):
            at[(d % 2 + k) % 2, d // 2, :, rows] = vt[d * RB : (d + 1) * RB]

    barrier = pltpu.get_barrier_semaphore()
    for to in (sib, xn, yn):
        signal(barrier, to)
    pl.semaphore_wait(barrier, 3)

    gather_own(0)
    load_x = pltpu.make_async_copy(x_hbm, h, in_sem.at[0])
    load_dy = pltpu.make_async_copy(dy_hbm, dy, in_sem.at[1])
    load_x.start()
    load_dy.start()
    load_x.wait()
    load_dy.wait()

    acc[...] = jnp.zeros_like(acc)

    @pl.loop(0, T // VB)
    def _(t):
        rows = tokens(t, VB)
        set_a(rows, h[rows, :].astype(f32))
        dyt[:, rows] = dy[rows, :].T

    gather_forward(0)
    gather_own(1)
    gather_last(0)
    gather_done(0)
    load_weights(0, 0)

    @pl.loop(0, CH)
    def _(c):
        slot = c % 2
        weights_loaded(slot)

        @pl.loop(0, T // TB)
        def _(t):
            rows = tokens(t, TB)
            gate = dot(a[rows, :], wg[slot])
            up = dot(a[rows, :], wu[slot])
            prod = (gate * jax.nn.sigmoid(gate) * up).astype(bf16)
            acc[:, rows] += dot_nt(wd[slot], prod)

            @pl.when(t == 1)
            def _():
                gather_forward(c + 1)
                gather_own(c + 2)

        gather_last(c + 1)
        gather_done(c + 1)
        load_weights(c + 1, (c + 1) % 2)

    @pl.loop(0, T // VB)
    def _(t):
        rows = tokens(t, VB)
        y = acc[:, rows].T.astype(bf16)
        v = (h[rows, :].astype(f32) + y.astype(f32)).astype(bf16)
        h[rows, :] = v
        set_a(rows, v.astype(f32))

    @pl.loop(0, LAYERS)
    def _(li):
        acc[...] = jnp.zeros_like(acc)

        @pl.loop(0, CH)
        def _(c):
            s = li * CH + c
            slot = c % 2
            weights_loaded(slot)

            @pl.loop(0, T // TB)
            def _(t):
                rows = tokens(t, TB)
                gate = dot(a[rows, :], wg[slot])
                up = dot(a[rows, :], wu[slot])
                dz = dot(dy[rows, :], wd[slot]).astype(bf16).astype(f32)
                sig = jax.nn.sigmoid(gate)
                act = gate * sig
                z[rows, :] = (act * up).astype(bf16)
                du[rows, :] = (dz * act).astype(bf16)
                dg[rows, :] = (dz * up * (sig + act * (1.0 - sig))).astype(bf16)

                @pl.when((t == 1) & (s < CH - 1))
                def _():
                    gather_forward(CH + c + 1)

                @pl.when((t == 1) & (s < CH - 2))
                def _():
                    gather_own(CH + c + 2)

            @pl.when(s > 0)
            def _():
                scatter_block(s - 1)
                for copy in sib_copies():
                    copy.wait_send()

            for m, grad in enumerate((dg, du)):

                @pl.loop(0, F // TB)
                def _(n):
                    cols = tokens(n, TB)
                    w = dot(at[...].reshape(D, T), grad[:, cols])
                    owng[m, :, :, cols] = w[:HD].reshape(4, RB, TB)
                    sibg[m, :, :, cols] = w[HD:].reshape(4, RB, TB).astype(bf16)

            @pl.loop(0, F // TB)
            def _(n):
                w = dot(dyt[...], z[:, tokens(n, TB)])
                for i in range(TB // (2 * CB)):
                    lo, hi = w[:, 2 * CB * i : 2 * CB * i + CB], w[:, 2 * CB * i + CB : 2 * CB * (i + 1)]
                    q = n * (TB // (2 * CB)) + i
                    ownd[q] = jnp.where(k == 0, lo, hi)
                    sibd[q] = jnp.where(k == 0, hi, lo).astype(bf16)

            scatter_sib(s)

            @pl.when(s < CH - 1)
            def _():
                gather_last(CH + c + 1)
                gather_done(CH + c + 1)

            @pl.when(s < STEPS - 1)
            def _():
                load_weights((CH + s + 1) % STEPS, (c + 1) % 2)

            @pl.loop(0, T // TB)
            def _(t):
                rows = tokens(t, TB)
                acc[:, rows] += dot_nt(wg[slot], dg[rows, :]) + dot_nt(wu[slot], du[rows, :])

            @pl.when(s > 0)
            def _():
                scatter_final(s - 1)

            scatter_diag(s)

        @pl.loop(0, T // VB)
        def _(t):
            rows = tokens(t, VB)
            da = acc[:, rows].T.astype(bf16).astype(f32)
            wide = h[rows, :].astype(f32)
            scale = scale_of(wide)
            along = jnp.mean(da * wide, -1, keepdims=True)
            dwide = (da * scale - wide * (along * scale * scale * scale)).astype(bf16)
            v = (dy[rows, :].astype(f32) + dwide.astype(f32)).astype(bf16)
            dy[rows, :] = v

        @pl.when(li == 0)
        def _():
            again = pltpu.make_async_copy(x_hbm, h, in_sem.at[0])
            again.start()

            @pl.loop(0, T // VB)
            def _(t):
                rows = tokens(t, VB)
                dyt[:, rows] = dy[rows, :].T

            again.wait()

            @pl.loop(0, T // VB)
            def _(t):
                rows = tokens(t, VB)
                set_a(rows, h[rows, :].astype(f32))

    store_dx = pltpu.make_async_copy(dy, dx_hbm, in_sem.at[1])
    store_dx.start()
    last = STEPS - 1
    scatter_block(last)
    scatter_final(last)
    for copy in sib_copies() + diag_copies() + block_copies():
        copy.wait_send()
    for copy in out_copies(CH - 1):
        copy.wait()
    for copy in (*own_copies(last), *forward_copies(last), *last_copies(last)):
        copy.wait_send()
    store_dx.wait()


def on_device(x, dy, gu_own, dn_own):
    hbm = pl.BlockSpec(memory_space=pl.ANY)
    shapes = (
        jax.ShapeDtypeStruct((T, D), bf16),
        jax.ShapeDtypeStruct((STEPS, 2, RB, F), bf16),
        jax.ShapeDtypeStruct((STEPS, D, CB), bf16),
        jax.ShapeDtypeStruct((STEPS, N, 2, RB, F), bf16),
        jax.ShapeDtypeStruct((STEPS, N, D, CB), bf16),
    )
    act = pltpu.VMEM((T, D), bf16)
    wide = pltpu.VMEM((T, F), bf16)
    block = [pltpu.VMEM((2, RB, F), bf16), pltpu.VMEM((D, CB), bf16)]
    scratch = [
        *[pltpu.VMEM((2, D, F), bf16)] * 3,
        act, act, pltpu.VMEM((2, 4, RB, T), bf16), act, pltpu.VMEM((D, T), bf16),
        wide, wide, wide, pltpu.VMEM((D, T), f32),
        pltpu.VMEM((2, 4, RB, F), f32), pltpu.VMEM((4, D, CB), f32),
        *[pltpu.VMEM((2, 4, RB, F), bf16), pltpu.VMEM((4, D, CB), bf16)] * 2,
        *block * 6,
        pltpu.VMEM((2, RB, F), f32), pltpu.VMEM((D, CB), f32), *block,
        pltpu.SemaphoreType.DMA((16,)),
        pltpu.SemaphoreType.DMA((STEPS, 16)),
        pltpu.SemaphoreType.DMA((2, 3)),
        pltpu.SemaphoreType.DMA((10,)),
        pltpu.SemaphoreType.DMA((10,)),
        pltpu.SemaphoreType.DMA((2,)),
        pltpu.SemaphoreType.DMA((2,)),
        pltpu.SemaphoreType.REGULAR,
        pltpu.SemaphoreType.REGULAR((2,)),
        pltpu.SemaphoreType.REGULAR((2,)),
    ]
    return pl.pallas_call(
        kernel,
        out_shape=shapes,
        in_specs=[hbm] * 4,
        out_specs=[hbm] * 5,
        scratch_shapes=scratch,
        compiler_params=pltpu.CompilerParams(collective_id=0, has_side_effects=True, vmem_limit_bytes=67_000_000),
        name="layers",
    )(x, dy, gu_own, dn_own)[:3]


def solution(mesh):
    def step(x, dy, w_gate, w_up, w_down):
        def cols(w):
            return w.reshape(LAYERS, RB, N, CH, CB).transpose(0, 3, 1, 2, 4).reshape(LAYERS, CH, RB, F)

        gu = jnp.stack((cols(w_gate), cols(w_up)), 2).reshape(STEPS, 2, RB, F)
        down = w_down.reshape(LAYERS, CH, CB, D).transpose(0, 1, 3, 2).reshape(STEPS, D, CB)
        dx, outg, outd = on_device(x[0], dy[0], gu, down)
        outg = outg.reshape(LAYERS, CH, 2, RB, N, CB).transpose(2, 0, 3, 4, 1, 5).reshape(2, LAYERS, RB, FF)
        outd = outd.reshape(LAYERS, CH, D, CB).transpose(0, 1, 3, 2).reshape(LAYERS, CH * CB, D)
        return dx[None], outg[0], outg[1], outd

    act, weight = P(("rep", "dp")), P(None, "dp")
    return jax.shard_map(
        step,
        mesh=mesh,
        in_specs=(act, act, weight, weight, weight),
        out_specs=(act, P("rep", "dp"), P("rep", "dp"), P("rep", "dp")),
        check_vma=False,
    )
```

time: 822 us -> 400 us (0.49)
  Pallas kernels: 0 us -> 370 us
  matrix products: 356 us -> 0 us
  waiting for transfers between devices: 311 us -> 0 us
  other arithmetic: 105 us -> 1.72 us
  between operations: 14.9 us -> 0.71 us
    pallas_call x0 -> x1, Pallas kernels: none -> 370 us  [on_device(): pl.pallas_call(kernel, out_shape=shapes, in_specs=[hbm] * 4, out_specs=[h...]
    dot_general x17 -> x0, matrix products: 356 us -> none  [the longest x6 137 us: layer(): up = jnp.dot(a, w['w_up'], preferred_element_type=jnp.float32)]
    unnamed x18 -> x0, waiting for transfers between devices: 229 us -> none
    unnamed x3 -> x0, other arithmetic: 87.7 us -> none
    squeeze x6 -> x0, waiting for transfers between devices: 82.4 us -> none  [stack(): h = layer(h, {name: w[number] for name, w in weights.items()})]
    unnamed x31 -> x4, local copies, waits for them, and re-layouts: 20.4 us -> 3.88 us
    reshape x0 -> x5, local copies, waits for them, and re-layouts: none -> 10.3 us  [the longest x4 7.85 us: cols(): w.reshape(LAYERS, RB, N, CH, CB).transpose(0, 3, 1, 2, 4)]
    broadcast_in_dim x6 -> x0, other arithmetic: 8.3 us -> none  [stack(): h = layer(h, {name: w[number] for name, w in weights.items()})]
  transfers between devices with their start and end apart: 12 -> 0, of which waited for: 9 -> 0; matrix products, arithmetic and copies ran while one was open for 45% -> 0% of each run, Pallas kernels for 0% -> 0%
where the time goes in v1:
time: 400 us
  Pallas kernels  370 us (92%)
  local copies, waits for them, and re-layouts  26.9 us (7%)
    pallas_call x1, Pallas kernels, on_device(): pl.pallas_call(kernel, out_shape=shapes, in_specs=[hbm] * 4, out_specs=[h...  370 us

profile of v1, /device:TPU:0, one launch (start us, length us, event | category | flops | bytes accessed | tf_op | source)
XLA Modules:
  0.0 399.5 jit_solution(3278582518595472999)
XLA Ops:
  0.6 3.2 reshape.39
  3.9 0.2 copy.19
  4.0 0.6 stack.7
  4.7 3.2 reshape.40
  7.9 1.2 copy.18
  9.1 2.4 stack.8
  11.5 1.7 pad_maximum_fusion.gu_own
  13.2 2.4 copy.11
  15.6 370.2 %layers.1 = (bf16[2048,640]{1,0:T(8,128)(2,1)}, bf16[8,2,80,1024]{3,2,1,0:T(8,128)(2,1)}, bf16[8,640,128]{2,1,0:T(8,128)(2,1)}, bf16[8,8,2,80,1024]{4,3,2,1,0:T(8,128)(2,1)}, bf16[8,8,640,128]{3,2,1,0:T(8,128)(2,1)}) custom-call(bf16[2048,640]{1,0:T(8,128)(2,1)} %bitcast.34, bf16[2048,640]{1,0:T(8,128)(2,1)} %bitcast.35, ...), custom_call_target="tpu_custom_call" | custom-call | tf_op jit(solution)/shard_map/layers/pallas_call | solution.py:481
  385.8 2.4 copy.15
  388.2 0.2 fusion
  388.4 1.7 copy.13
  390.1 1.8 squeeze.15
  391.9 1.7 copy.12
  393.6 1.8 squeeze.14
  395.5 0.0 copy-start
  395.5 2.6 copy.14
  398.0 0.0 copy-done
  398.0 1.5 copy.21
Async XLA Ops:
  395.5 2.6 copy-start

commit v2 on v1

--- a/solution.py
+++ b/solution.py
@@ -15,6 +15,7 @@
 STEPS = LAYERS * CH
 TB = 512
 VB = 256
+TILES = T // VB
 
 f32, bf16 = jnp.float32, jnp.bfloat16
 
@@ -28,12 +29,13 @@
 
 
 def kernel(
-    x_hbm, dy_hbm, gu_own, dn_own,
-    dx_hbm, outg_hbm, outd_hbm, gu_all, dn_all,
+    x_hbm, dy_hbm, wg_hbm, wu_hbm, wd_hbm,
+    dx_hbm, outg_hbm, outu_hbm, outd_hbm, gu_all, dn_all, saved_hbm, z_hbm,
     wg, wu, wd, h, a, at, dy, dyt, z, dg, du, acc,
     owng, ownd, sibg, sibd, recg, recd, sdg, sdd, rdg, rdd,
     sxg, sxd, syg, syd, bxg, bxd, byg, byd, fing, find, og, od,
-    ag_send, ag_recv, load_sem, rs_send, rs_recv, out_sem, in_sem, free_sib, free_diag, free_block,
+    packed, dn_own, saved,
+    ag_send, ag_recv, load_sem, rs_send, rs_recv, out_sem, in_sem, pack_sem, saved_sem, z_sem, free_sib, free_diag, free_block,
 ):
     me = lax.axis_index("dp")
     k = me % 2
@@ -54,11 +56,23 @@
     def signal(sem, to):
         pl.semaphore_signal(sem, inc=1, device_id={"dp": to}, device_id_type=pl.DeviceIdType.MESH)
 
-    def own_copies(j):
+    def own_gu(j):
         for i, to in enumerate((xn, yn, sib)):
-            r = (0, 2, 8)[i]
-            yield far(gu_own.at[j], gu_all.at[j, me], ag_send.at[2 * i], ag_recv.at[j, r], to)
-            yield far(dn_own.at[j], dn_all.at[j, me], ag_send.at[2 * i + 1], ag_recv.at[j, r + 1], to)
+            yield far(packed.at[j % 2], gu_all.at[j, me], ag_send.at[2 * i], ag_recv.at[j, (0, 2, 8)[i]], to)
+
+    def own_dn(j):
+        for i, to in enumerate((xn, yn, sib)):
+            yield far(dn_own.at[j], dn_all.at[j, me], ag_send.at[2 * i + 1], ag_recv.at[j, (1, 3, 9)[i]], to)
+
+    def slabs(j):
+        layer, c = j // CH, j % CH
+        for d in range(N):
+            yield layer, pl.ds(pl.multiple_of(CH * CB * d + CB * c, CB), CB), pl.ds(CB * d, CB)
+
+    def pack(j):
+        for layer, there, here in slabs(j):
+            for m, w in enumerate((wg_hbm, wu_hbm)):
+                pltpu.make_async_copy(w.at[layer, :, there], packed.at[j % 2, m, :, here], pack_sem.at[j % 2]).start()
 
     def forward_copies(j):
         top, bot = pl.ds(0, HD), pl.ds(HD, HD)
@@ -77,14 +91,29 @@
     def arrived(ref, j, r, frm):
         far(ref, ref, ag_send.at[0], ag_recv.at[j, r], frm).wait_recv()
 
-    def gather_own(j):
+    def gather_own_dn(j):
         @pl.when(j > 0)
         def _():
-            for copy in own_copies(j):
+            for copy in own_dn(j):
                 copy.wait_send()
 
-        for copy in own_copies(j):
+        for copy in own_dn(j):
             copy.start()
+
+    def gather_own_gu(j):
+        pltpu.make_async_copy(packed.at[j % 2], packed.at[j % 2], pack_sem.at[j % 2]).wait()
+
+        @pl.when(j > 0)
+        def _():
+            for copy in own_gu(j):
+                copy.wait_send()
+
+        for copy in own_gu(j):
+            copy.start()
+
+        @pl.when((j > 0) & (j < STEPS - 1))
+        def _():
+            pack(j + 1)
 
     def gather_forward(j):
         arrived(gu_all.at[j, xn], j, 0, xn)
@@ -123,17 +152,21 @@
             arrived(dn_all.at[j, src], j, r + 1, sib)
 
     def load_weights(j, slot):
-        def parts(gu, down, src):
-            rows = pl.ds(pl.multiple_of(src * RB, RB), RB)
-            cols = pl.ds(pl.multiple_of(src * CB, CB), CB)
-            pltpu.make_async_copy(gu.at[0], wg.at[slot, rows], load_sem.at[slot, 0]).start()
-            pltpu.make_async_copy(gu.at[1], wu.at[slot, rows], load_sem.at[slot, 1]).start()
-            pltpu.make_async_copy(down, wd.at[slot, :, cols], load_sem.at[slot, 2]).start()
-
-        parts(gu_own.at[j], dn_own.at[j], me)
+        def rows(src):
+            return pl.ds(pl.multiple_of(src * RB, RB), RB)
+
+        def cols(src):
+            return pl.ds(pl.multiple_of(src * CB, CB), CB)
+
+        for layer, there, here in slabs(j):
+            for m, (w, to) in enumerate(((wg_hbm, wg), (wu_hbm, wu))):
+                pltpu.make_async_copy(w.at[layer, :, there], to.at[slot, rows(me), here], load_sem.at[slot, m]).start()
+        pltpu.make_async_copy(dn_own.at[j], wd.at[slot, :, cols(me)], load_sem.at[slot, 2]).start()
         for i in range(1, N):
             src = (me + i) % N
-            parts(gu_all.at[j, src], dn_all.at[j, src], src)
+            pltpu.make_async_copy(gu_all.at[j, src, 0], wg.at[slot, rows(src)], load_sem.at[slot, 0]).start()
+            pltpu.make_async_copy(gu_all.at[j, src, 1], wu.at[slot, rows(src)], load_sem.at[slot, 1]).start()
+            pltpu.make_async_copy(dn_all.at[j, src], wd.at[slot, :, cols(src)], load_sem.at[slot, 2]).start()
 
     def weights_loaded(slot):
         for i, w in enumerate((wg, wu, wd)):
@@ -162,11 +195,16 @@
             far(syd, byd, rs_send.at[9], rs_recv.at[9], yn),
         )
 
-    def out_copies(j):
-        return (
-            pltpu.make_async_copy(og, outg_hbm.at[j], out_sem.at[0]),
-            pltpu.make_async_copy(od, outd_hbm.at[j], out_sem.at[1]),
-        )
+    def store_out(j):
+        for layer, there, here in slabs(j):
+            for m, out in enumerate((outg_hbm, outu_hbm)):
+                pltpu.make_async_copy(og.at[m, :, here], out.at[layer, :, there], out_sem.at[0]).start()
+        rows = pl.ds(pl.multiple_of(j % CH * CB, CB), CB)
+        pltpu.make_async_copy(od, outd_hbm.at[j // CH, rows], out_sem.at[1]).start()
+
+    def out_stored():
+        pltpu.make_async_copy(og, og, out_sem.at[0]).wait()
+        pltpu.make_async_copy(od, od, out_sem.at[1]).wait()
 
     def scatter_sib(s):
         @pl.when(s > 0)
@@ -242,22 +280,20 @@
 
         @pl.when(s > 0)
         def _():
-            for copy in out_copies(j):
-                copy.wait()
+            out_stored()
 
         for copy in block_copies():
             copy.wait_recv()
         for m in range(2):
             og[m] = (fing[m] + bxg[m].astype(f32) + byg[m].astype(f32)).astype(bf16)
-        od[...] = (find[...] + bxd[...].astype(f32) + byd[...].astype(f32)).astype(bf16)
+        od[...] = (find[...] + bxd[...].astype(f32) + byd[...].astype(f32)).T.astype(bf16)
 
         @pl.when(s < STEPS - 1)
         def _():
             signal(free_block.at[0], xn)
             signal(free_block.at[1], yn)
 
-        for copy in out_copies(j):
-            copy.start()
+        store_out(j)
 
     def scale_of(wide):
         return lax.rsqrt(jnp.mean(wide * wide, -1, keepdims=True) + 1e-6)
@@ -272,19 +308,37 @@
         for d in range(N):
             at[(d % 2 + k) % 2, d // 2, :, rows] = vt[d * RB : (d + 1) * RB]
 
+    def store_saved(c, t):
+        return pltpu.make_async_copy(saved.at[t % 2], saved_hbm.at[c, t], saved_sem.at[t % 2])
+
+    def load_saved(n):
+        return pltpu.make_async_copy(saved_hbm.at[n // TILES, n % TILES], saved.at[n % 2], saved_sem.at[n % 2])
+
+    pack(0)
+    pack(1)
+    raw = a.at[pl.ds(0, LAYERS * CH * CB)]
+    load_dn = [pltpu.make_async_copy(wd_hbm.at[i], raw.at[pl.ds(i * CH * CB, CH * CB)], in_sem.at[2 + i]) for i in range(LAYERS)]
+    load_x = pltpu.make_async_copy(x_hbm.at[0], h, in_sem.at[0])
+    load_dy = pltpu.make_async_copy(dy_hbm.at[0], dy, in_sem.at[1])
+    for copy in (*load_dn, load_x, load_dy):
+        copy.start()
     barrier = pltpu.get_barrier_semaphore()
     for to in (sib, xn, yn):
         signal(barrier, to)
     pl.semaphore_wait(barrier, 3)
 
-    gather_own(0)
-    load_x = pltpu.make_async_copy(x_hbm, h, in_sem.at[0])
-    load_dy = pltpu.make_async_copy(dy_hbm, dy, in_sem.at[1])
-    load_x.start()
-    load_dy.start()
+    gather_own_gu(0)
+    for copy in load_dn:
+        copy.wait()
+
+    @pl.loop(0, STEPS)
+    def _(j):
+        dn_own[j] = a[tokens(j, CB), :].T
+
+    gather_own_dn(0)
+    gather_own_dn(1)
     load_x.wait()
     load_dy.wait()
-
     acc[...] = jnp.zeros_like(acc)
 
     @pl.loop(0, T // VB)
@@ -294,7 +348,7 @@
         dyt[:, rows] = dy[rows, :].T
 
     gather_forward(0)
-    gather_own(1)
+    gather_own_gu(1)
     gather_last(0)
     gather_done(0)
     load_weights(0, 0)
@@ -304,18 +358,39 @@
         slot = c % 2
         weights_loaded(slot)
 
+        @pl.when(c > 0)
+        def _():
+            pltpu.make_async_copy(z, z_hbm.at[c], z_sem).wait()
+
+        @pl.loop(0, TILES)
+        def _(t):
+            rows = tokens(t, VB)
+
+            @pl.when(c * TILES + t > 1)
+            def _():
+                store_saved(c, t).wait()
+
+            gate = dot(a[rows, :], wg[slot])
+            up = dot(a[rows, :], wu[slot])
+            sig = jax.nn.sigmoid(gate)
+            act = gate * sig
+            z[rows, :] = (act * up).astype(bf16)
+            saved[t % 2, 0] = act
+            saved[t % 2, 1] = up * (sig + act * (1.0 - sig))
+            store_saved(c, t).start()
+
+            @pl.when(t == 1)
+            def _():
+                gather_own_dn(c + 2)
+                gather_forward(c + 1)
+                gather_own_gu(c + 2)
+
+        pltpu.make_async_copy(z, z_hbm.at[c], z_sem).start()
+
         @pl.loop(0, T // TB)
         def _(t):
             rows = tokens(t, TB)
-            gate = dot(a[rows, :], wg[slot])
-            up = dot(a[rows, :], wu[slot])
-            prod = (gate * jax.nn.sigmoid(gate) * up).astype(bf16)
-            acc[:, rows] += dot_nt(wd[slot], prod)
-
-            @pl.when(t == 1)
-            def _():
-                gather_forward(c + 1)
-                gather_own(c + 2)
+            acc[:, rows] += dot_nt(wd[slot], z[rows, :])
 
         gather_last(c + 1)
         gather_done(c + 1)
@@ -329,6 +404,12 @@
         h[rows, :] = v
         set_a(rows, v.astype(f32))
 
+    pltpu.make_async_copy(z, z_hbm.at[CH - 1], z_sem).wait()
+    for t in (0, 1):
+        store_saved(CH - 1, t).wait()
+    for t in (0, 1):
+        load_saved(t).start()
+
     @pl.loop(0, LAYERS)
     def _(li):
         acc[...] = jnp.zeros_like(acc)
@@ -339,25 +420,45 @@
             slot = c % 2
             weights_loaded(slot)
 
-            @pl.loop(0, T // TB)
-            def _(t):
-                rows = tokens(t, TB)
-                gate = dot(a[rows, :], wg[slot])
-                up = dot(a[rows, :], wu[slot])
-                dz = dot(dy[rows, :], wd[slot]).astype(bf16).astype(f32)
-                sig = jax.nn.sigmoid(gate)
-                act = gate * sig
-                z[rows, :] = (act * up).astype(bf16)
-                du[rows, :] = (dz * act).astype(bf16)
-                dg[rows, :] = (dz * up * (sig + act * (1.0 - sig))).astype(bf16)
-
-                @pl.when((t == 1) & (s < CH - 1))
-                def _():
-                    gather_forward(CH + c + 1)
-
-                @pl.when((t == 1) & (s < CH - 2))
-                def _():
-                    gather_own(CH + c + 2)
+            @pl.when(li == 0)
+            def _():
+                @pl.loop(0, T // TB)
+                def _(t):
+                    rows = tokens(t, TB)
+                    gate = dot(a[rows, :], wg[slot])
+                    up = dot(a[rows, :], wu[slot])
+                    dz = dot(dy[rows, :], wd[slot]).astype(bf16).astype(f32)
+                    sig = jax.nn.sigmoid(gate)
+                    act = gate * sig
+                    z[rows, :] = (act * up).astype(bf16)
+                    du[rows, :] = (dz * act).astype(bf16)
+                    dg[rows, :] = (dz * (up * (sig + act * (1.0 - sig)))).astype(bf16)
+
+                    @pl.when((t == 0) & (s == 0))
+                    def _():
+                        gather_own_dn(CH + 2)
+                        gather_forward(CH + 1)
+                        gather_own_gu(CH + 2)
+
+                    @pl.when((t == 0) & (s == 1))
+                    def _():
+                        gather_last(CH + 2)
+                        gather_forward(CH + 3)
+
+            @pl.when(li > 0)
+            def _():
+                @pl.loop(0, TILES)
+                def _(t):
+                    rows = tokens(t, VB)
+                    n = c * TILES + t
+                    dz = dot(dy[rows, :], wd[slot]).astype(bf16).astype(f32)
+                    load_saved(n).wait()
+                    du[rows, :] = (dz * saved[t % 2, 0]).astype(bf16)
+                    dg[rows, :] = (dz * saved[t % 2, 1]).astype(bf16)
+
+                    @pl.when(n < CH * TILES - 2)
+                    def _():
+                        load_saved(n + 2).start()
 
             @pl.when(s > 0)
             def _():
@@ -373,6 +474,10 @@
                     w = dot(at[...].reshape(D, T), grad[:, cols])
                     owng[m, :, :, cols] = w[:HD].reshape(4, RB, TB)
                     sibg[m, :, :, cols] = w[HD:].reshape(4, RB, TB).astype(bf16)
+
+            @pl.when(li > 0)
+            def _():
+                pltpu.make_async_copy(z_hbm.at[c], z, z_sem).wait()
 
             @pl.loop(0, F // TB)
             def _(n):
@@ -385,10 +490,26 @@
 
             scatter_sib(s)
 
-            @pl.when(s < CH - 1)
-            def _():
-                gather_last(CH + c + 1)
-                gather_done(CH + c + 1)
+            @pl.when((s >= CH - 1) & (s < STEPS - 1))
+            def _():
+                pltpu.make_async_copy(z_hbm.at[s - (CH - 1)], z, z_sem).start()
+
+            @pl.when(s == 0)
+            def _():
+                gather_last(CH + 1)
+                gather_done(CH + 1)
+                gather_own_dn(CH + 3)
+                gather_forward(CH + 2)
+                gather_own_gu(CH + 3)
+
+            @pl.when(s == 1)
+            def _():
+                gather_done(CH + 2)
+                gather_last(CH + 3)
+
+            @pl.when(s == 2)
+            def _():
+                gather_done(CH + 3)
 
             @pl.when(s < STEPS - 1)
             def _():
@@ -399,11 +520,13 @@
                 rows = tokens(t, TB)
                 acc[:, rows] += dot_nt(wg[slot], dg[rows, :]) + dot_nt(wu[slot], du[rows, :])
 
-            @pl.when(s > 0)
-            def _():
-                scatter_final(s - 1)
-
-            scatter_diag(s)
+                @pl.when((t == 2) & (s > 0))
+                def _():
+                    scatter_final(s - 1)
+
+                @pl.when(t == 2)
+                def _():
+                    scatter_diag(s)
 
         @pl.loop(0, T // VB)
         def _(t):
@@ -415,17 +538,16 @@
             dwide = (da * scale - wide * (along * scale * scale * scale)).astype(bf16)
             v = (dy[rows, :].astype(f32) + dwide.astype(f32)).astype(bf16)
             dy[rows, :] = v
+            dyt[:, rows] = v.T
+
+            @pl.when((li > 0) & (t == 3))
+            def _():
+                scatter_block(STEPS - 1)
 
         @pl.when(li == 0)
         def _():
-            again = pltpu.make_async_copy(x_hbm, h, in_sem.at[0])
+            again = pltpu.make_async_copy(x_hbm.at[0], h, in_sem.at[0])
             again.start()
-
-            @pl.loop(0, T // VB)
-            def _(t):
-                rows = tokens(t, VB)
-                dyt[:, rows] = dy[rows, :].T
-
             again.wait()
 
             @pl.loop(0, T // VB)
@@ -433,79 +555,64 @@
                 rows = tokens(t, VB)
                 set_a(rows, h[rows, :].astype(f32))
 
-    store_dx = pltpu.make_async_copy(dy, dx_hbm, in_sem.at[1])
+    store_dx = pltpu.make_async_copy(dy, dx_hbm.at[0], in_sem.at[1])
     store_dx.start()
     last = STEPS - 1
-    scatter_block(last)
     scatter_final(last)
     for copy in sib_copies() + diag_copies() + block_copies():
         copy.wait_send()
-    for copy in out_copies(CH - 1):
-        copy.wait()
-    for copy in (*own_copies(last), *forward_copies(last), *last_copies(last)):
+    out_stored()
+    for copy in (*own_gu(last), *own_dn(last), *forward_copies(last), *last_copies(last)):
         copy.wait_send()
     store_dx.wait()
 
 
-def on_device(x, dy, gu_own, dn_own):
+def on_device(x, dy, w_gate, w_up, w_down):
     hbm = pl.BlockSpec(memory_space=pl.ANY)
     shapes = (
-        jax.ShapeDtypeStruct((T, D), bf16),
-        jax.ShapeDtypeStruct((STEPS, 2, RB, F), bf16),
-        jax.ShapeDtypeStruct((STEPS, D, CB), bf16),
+        jax.ShapeDtypeStruct((1, T, D), bf16),
+        jax.ShapeDtypeStruct((LAYERS, RB, FF), bf16),
+        jax.ShapeDtypeStruct((LAYERS, RB, FF), bf16),
+        jax.ShapeDtypeStruct((LAYERS, CH * CB, D), bf16),
         jax.ShapeDtypeStruct((STEPS, N, 2, RB, F), bf16),
         jax.ShapeDtypeStruct((STEPS, N, D, CB), bf16),
+        jax.ShapeDtypeStruct((CH, TILES, 2, VB, F), f32),
+        jax.ShapeDtypeStruct((CH, T, F), bf16),
     )
     act = pltpu.VMEM((T, D), bf16)
     wide = pltpu.VMEM((T, F), bf16)
-    block = [pltpu.VMEM((2, RB, F), bf16), pltpu.VMEM((D, CB), bf16)]
+    gu, down = pltpu.VMEM((2, RB, F), bf16), pltpu.VMEM((D, CB), bf16)
+    dma = pltpu.SemaphoreType.DMA
     scratch = [
         *[pltpu.VMEM((2, D, F), bf16)] * 3,
         act, act, pltpu.VMEM((2, 4, RB, T), bf16), act, pltpu.VMEM((D, T), bf16),
         wide, wide, wide, pltpu.VMEM((D, T), f32),
         pltpu.VMEM((2, 4, RB, F), f32), pltpu.VMEM((4, D, CB), f32),
         *[pltpu.VMEM((2, 4, RB, F), bf16), pltpu.VMEM((4, D, CB), bf16)] * 2,
-        *block * 6,
-        pltpu.VMEM((2, RB, F), f32), pltpu.VMEM((D, CB), f32), *block,
-        pltpu.SemaphoreType.DMA((16,)),
-        pltpu.SemaphoreType.DMA((STEPS, 16)),
-        pltpu.SemaphoreType.DMA((2, 3)),
-        pltpu.SemaphoreType.DMA((10,)),
-        pltpu.SemaphoreType.DMA((10,)),
-        pltpu.SemaphoreType.DMA((2,)),
-        pltpu.SemaphoreType.DMA((2,)),
-        pltpu.SemaphoreType.REGULAR,
-        pltpu.SemaphoreType.REGULAR((2,)),
-        pltpu.SemaphoreType.REGULAR((2,)),
+        *[gu, down] * 6,
+        pltpu.VMEM((2, RB, F), f32), pltpu.VMEM((D, CB), f32), gu, pltpu.VMEM((CB, D), bf16),
+        pltpu.VMEM((2, 2, RB, F), bf16), pltpu.VMEM((STEPS, D, CB), bf16), pltpu.VMEM((2, 2, VB, F), f32),
+        dma((16,)), dma((STEPS, 16)), dma((2, 3)), dma((10,)), dma((10,)), dma((2,)), dma((4,)), dma((2,)), dma((2,)), dma,
+        pltpu.SemaphoreType.REGULAR, pltpu.SemaphoreType.REGULAR((2,)), pltpu.SemaphoreType.REGULAR((2,)),
     ]
     return pl.pallas_call(
         kernel,
         out_shape=shapes,
-        in_specs=[hbm] * 4,
-        out_specs=[hbm] * 5,
+        in_specs=[hbm] * 5,
+        out_specs=[hbm] * 8,
         scratch_shapes=scratch,
         compiler_params=pltpu.CompilerParams(collective_id=0, has_side_effects=True, vmem_limit_bytes=67_000_000),
         name="layers",
-    )(x, dy, gu_own, dn_own)[:3]
+    )(x, dy, w_gate, w_up, w_down)[:4]
 
 
 def solution(mesh):
-    def step(x, dy, w_gate, w_up, w_down):
-        def cols(w):
-            return w.reshape(LAYERS, RB, N, CH, CB).transpose(0, 3, 1, 2, 4).reshape(LAYERS, CH, RB, F)
-
-        gu = jnp.stack((cols(w_gate), cols(w_up)), 2).reshape(STEPS, 2, RB, F)
-        down = w_down.reshape(LAYERS, CH, CB, D).transpose(0, 1, 3, 2).reshape(STEPS, D, CB)
-        dx, outg, outd = on_device(x[0], dy[0], gu, down)
-        outg = outg.reshape(LAYERS, CH, 2, RB, N, CB).transpose(2, 0, 3, 4, 1, 5).reshape(2, LAYERS, RB, FF)
-        outd = outd.reshape(LAYERS, CH, D, CB).transpose(0, 1, 3, 2).reshape(LAYERS, CH * CB, D)
-        return dx[None], outg[0], outg[1], outd
-
     act, weight = P(("rep", "dp")), P(None, "dp")
+    grad = P("rep", "dp")
     return jax.shard_map(
-        step,
+        on_device,
         mesh=mesh,
         in_specs=(act, act, weight, weight, weight),
-        out_specs=(act, P("rep", "dp"), P("rep", "dp"), P("rep", "dp")),
+        out_specs=(act, grad, grad, grad),
         check_vma=False,
     )

time: 400 us -> 357 us (0.89)
  Pallas kernels: 370 us -> 348 us
  local copies, waits for them, and re-layouts: 26.9 us -> 8.2 us
    pallas_call x1, Pallas kernels: 370 us -> 348 us  [on_device(): pl.pallas_call(kernel, out_shape=shapes, in_specs=[hbm] * 5, out_specs=[h...]
    reshape x5 -> x0, local copies, waits for them, and re-layouts: 10.3 us -> none  [the longest x4 7.85 us: cols(): w.reshape(LAYERS, RB, N, CH, CB).transpose(0, 3, 1, 2, 4)]
    unnamed x4 -> x10, local copies, waits for them, and re-layouts: 3.88 us -> 8.2 us
where the time goes in v2:
time: 357 us
  Pallas kernels  348 us (97%)
  local copies, waits for them, and re-layouts  8.2 us (2%)
    pallas_call x1, Pallas kernels, on_device(): pl.pallas_call(kernel, out_shape=shapes, in_specs=[hbm] * 5, out_specs=[h...  348 us
    unnamed x10, local copies, waits for them, and re-layouts  8.2 us

profile of v2, /device:TPU:0, one launch (start us, length us, event | category | flops | bytes accessed | tf_op | source)
XLA Modules:
  0.0 356.7 jit_solution(14355070955334488879)
XLA Ops:
  0.6 347.9 %layers.1 = (bf16[1,2048,640]{2,1,0:T(8,128)(2,1)}, bf16[2,80,4096]{2,1,0:T(8,128)(2,1)}, bf16[2,80,4096]{2,1,0:T(8,128)(2,1)}, bf16[2,512,640]{2,1,0:T(8,128)(2...) custom-call(bf16[1,2048,640]{2,1,0:T(8,128)(2,1)} %x_hbm.1, ...), custom_call_target="tpu_custom_call" | custom-call | tf_op jit(solution)/shard_map/layers/pallas_call | solution.py:598
  348.5 0.0 copy-start.2
  348.5 3.6 copy.13
  352.1 0.0 copy-done.2
  352.1 0.0 copy-start.1
  352.1 1.1 copy.14
  353.1 0.7 copy-done.1
  353.9 0.0 copy-start
  353.9 1.1 copy.15
  354.9 0.7 copy-done
  355.6 1.1 copy.16
Async XLA Ops:
  348.5 3.6 %copy-start.2 = (bf16[2,80,4096]{2,1,0:T(8,128)(2,1)S(1)}, bf16[2,80,4096]{2,1,0:T(8,128)(2,1)}, u32[]{:S(2)}) copy-start(bf16[2,80,4096]{2,1,0:T(8,128)(2,1)} %get-tuple-element.17) | copy-start | bytes 3932164
  352.1 1.8 copy-start.1
  353.9 1.8 copy-start

commit v3 on v2

--- a/solution.py
+++ b/solution.py
@@ -74,14 +74,17 @@
             for m, w in enumerate((wg_hbm, wu_hbm)):
                 pltpu.make_async_copy(w.at[layer, :, there], packed.at[j % 2, m, :, here], pack_sem.at[j % 2]).start()
 
-    def forward_copies(j):
+    def forward_gu(j):
+        yield far(gu_all.at[j, xn, 0], gu_all.at[j, xn, 0], ag_send.at[6], ag_recv.at[j, 4], yn)
+        yield far(gu_all.at[j, yn, 1], gu_all.at[j, yn, 1], ag_send.at[8], ag_recv.at[j, 6], xn)
+        for i, src in enumerate((xn, yn)):
+            yield far(gu_all.at[j, src], gu_all.at[j, src], ag_send.at[10 + 2 * i], ag_recv.at[j, 10 + 2 * i], sib)
+
+    def forward_dn(j):
         top, bot = pl.ds(0, HD), pl.ds(HD, HD)
-        yield far(gu_all.at[j, xn, 0], gu_all.at[j, xn, 0], ag_send.at[6], ag_recv.at[j, 4], yn)
         yield far(dn_all.at[j, xn, top], dn_all.at[j, xn, top], ag_send.at[7], ag_recv.at[j, 5], yn)
-        yield far(gu_all.at[j, yn, 1], gu_all.at[j, yn, 1], ag_send.at[8], ag_recv.at[j, 6], xn)
         yield far(dn_all.at[j, yn, bot], dn_all.at[j, yn, bot], ag_send.at[9], ag_recv.at[j, 7], xn)
         for i, src in enumerate((xn, yn)):
-            yield far(gu_all.at[j, src], gu_all.at[j, src], ag_send.at[10 + 2 * i], ag_recv.at[j, 10 + 2 * i], sib)
             yield far(dn_all.at[j, src], dn_all.at[j, src], ag_send.at[11 + 2 * i], ag_recv.at[j, 11 + 2 * i], sib)
 
     def last_copies(j):
@@ -115,19 +118,33 @@
         def _():
             pack(j + 1)
 
+    def gather_forward_gu(j):
+        arrived(gu_all.at[j, xn], j, 0, xn)
+        arrived(gu_all.at[j, yn], j, 2, yn)
+
+        @pl.when(j > 0)
+        def _():
+            for copy in forward_gu(j):
+                copy.wait_send()
+
+        for copy in forward_gu(j):
+            copy.start()
+
+    def gather_forward_dn(j):
+        arrived(dn_all.at[j, xn], j, 1, xn)
+        arrived(dn_all.at[j, yn], j, 3, yn)
+
+        @pl.when(j > 0)
+        def _():
+            for copy in forward_dn(j):
+                copy.wait_send()
+
+        for copy in forward_dn(j):
+            copy.start()
+
     def gather_forward(j):
-        arrived(gu_all.at[j, xn], j, 0, xn)
-        arrived(dn_all.at[j, xn], j, 1, xn)
-        arrived(gu_all.at[j, yn], j, 2, yn)
-        arrived(dn_all.at[j, yn], j, 3, yn)
-
-        @pl.when(j > 0)
-        def _():
-            for copy in forward_copies(j):
-                copy.wait_send()
-
-        for copy in forward_copies(j):
-            copy.start()
+        gather_forward_dn(j)
+        gather_forward_gu(j)
 
     def gather_last(j):
         top, bot = pl.ds(0, HD), pl.ds(HD, HD)
@@ -144,29 +161,34 @@
         for copy in last_copies(j):
             copy.start()
 
+    def gather_sib(j, which):
+        for i in which:
+            src = 2 * (chip, chip_x, chip_y, chip_d)[i] + (1 - k)
+            arrived(gu_all.at[j, src], j, 8 + 2 * i, sib)
+            arrived(dn_all.at[j, src], j, 9 + 2 * i, sib)
+
     def gather_done(j):
-        for i, c in enumerate((chip, chip_x, chip_y, chip_d)):
-            src = 2 * c + (1 - k)
-            r = 8 + 2 * i
-            arrived(gu_all.at[j, src], j, r, sib)
-            arrived(dn_all.at[j, src], j, r + 1, sib)
-
-    def load_weights(j, slot):
+        gather_sib(j, range(4))
+
+    def load_pieces(j, slot, sources, own=False):
         def rows(src):
             return pl.ds(pl.multiple_of(src * RB, RB), RB)
 
         def cols(src):
             return pl.ds(pl.multiple_of(src * CB, CB), CB)
 
-        for layer, there, here in slabs(j):
-            for m, (w, to) in enumerate(((wg_hbm, wg), (wu_hbm, wu))):
-                pltpu.make_async_copy(w.at[layer, :, there], to.at[slot, rows(me), here], load_sem.at[slot, m]).start()
-        pltpu.make_async_copy(dn_own.at[j], wd.at[slot, :, cols(me)], load_sem.at[slot, 2]).start()
-        for i in range(1, N):
-            src = (me + i) % N
+        for src in sources:
             pltpu.make_async_copy(gu_all.at[j, src, 0], wg.at[slot, rows(src)], load_sem.at[slot, 0]).start()
             pltpu.make_async_copy(gu_all.at[j, src, 1], wu.at[slot, rows(src)], load_sem.at[slot, 1]).start()
             pltpu.make_async_copy(dn_all.at[j, src], wd.at[slot, :, cols(src)], load_sem.at[slot, 2]).start()
+        if own:
+            for layer, there, here in slabs(j):
+                for m, (w, to) in enumerate(((wg_hbm, wg), (wu_hbm, wu))):
+                    pltpu.make_async_copy(w.at[layer, :, there], to.at[slot, rows(me), here], load_sem.at[slot, m]).start()
+            pltpu.make_async_copy(dn_own.at[j], wd.at[slot, :, cols(me)], load_sem.at[slot, 2]).start()
+
+    def load_weights(j, slot):
+        load_pieces(j, slot, [(me + i) % N for i in range(1, N)], own=True)
 
     def weights_loaded(slot):
         for i, w in enumerate((wg, wu, wd)):
@@ -174,26 +196,46 @@
 
     def sib_copies():
         return (
-            far(sibg, recg, rs_send.at[0], rs_recv.at[0], sib),
-            far(sibd, recd, rs_send.at[1], rs_recv.at[1], sib),
+            far(sibg.at[0], recg.at[0], rs_send.at[0], rs_recv.at[0], sib),
+            far(sibg.at[1], recg.at[1], rs_send.at[1], rs_recv.at[1], sib),
+            far(sibd, recd, rs_send.at[2], rs_recv.at[2], sib),
         )
 
-    def diag_copies():
+    def near_copies(which):
+        top, bot = pl.ds(0, HD), pl.ds(HD, HD)
+        if which == 0:
+            return (
+                far(sdg.at[0], rdg.at[0], rs_send.at[3], rs_recv.at[3], xn),
+                far(sxg.at[0], bxg.at[0], rs_send.at[4], rs_recv.at[4], xn),
+            )
+        if which == 1:
+            return (
+                far(sdg.at[1], rdg.at[1], rs_send.at[5], rs_recv.at[5], yn),
+                far(syg.at[1], byg.at[1], rs_send.at[6], rs_recv.at[6], yn),
+            )
+        return (
+            far(sdd.at[top], rdd.at[top], rs_send.at[7], rs_recv.at[7], xn),
+            far(sdd.at[bot], rdd.at[bot], rs_send.at[8], rs_recv.at[8], yn),
+            far(sxd.at[top], bxd.at[top], rs_send.at[9], rs_recv.at[9], xn),
+            far(syd.at[bot], byd.at[bot], rs_send.at[10], rs_recv.at[10], yn),
+        )
+
+    def sum_copies():
         top, bot = pl.ds(0, HD), pl.ds(HD, HD)
         return (
-            far(sdg.at[0], rdg.at[0], rs_send.at[2], rs_recv.at[2], xn),
-            far(sdd.at[top], rdd.at[top], rs_send.at[3], rs_recv.at[3], xn),
-            far(sdg.at[1], rdg.at[1], rs_send.at[4], rs_recv.at[4], yn),
-            far(sdd.at[bot], rdd.at[bot], rs_send.at[5], rs_recv.at[5], yn),
+            far(sxg.at[1], bxg.at[1], rs_send.at[11], rs_recv.at[11], xn),
+            far(syg.at[0], byg.at[0], rs_send.at[12], rs_recv.at[12], yn),
+            far(sxd.at[bot], bxd.at[bot], rs_send.at[13], rs_recv.at[13], xn),
+            far(syd.at[top], byd.at[top], rs_send.at[14], rs_recv.at[14], yn),
         )
 
-    def block_copies():
-        return (
-            far(sxg, bxg, rs_send.at[6], rs_recv.at[6], xn),
-            far(sxd, bxd, rs_send.at[7], rs_recv.at[7], xn),
-            far(syg, byg, rs_send.at[8], rs_recv.at[8], yn),
-            far(syd, byd, rs_send.at[9], rs_recv.at[9], yn),
-        )
+    def diag_arrived():
+        for copy in (near_copies(0)[0], near_copies(1)[0], *near_copies(2)[:2]):
+            copy.wait_recv()
+
+    def blocks_arrived():
+        for copy in (near_copies(0)[1], near_copies(1)[1], *near_copies(2)[2:], *sum_copies()):
+            copy.wait_recv()
 
     def store_out(j):
         for layer, there, here in slabs(j):
@@ -206,73 +248,73 @@
         pltpu.make_async_copy(og, og, out_sem.at[0]).wait()
         pltpu.make_async_copy(od, od, out_sem.at[1]).wait()
 
-    def scatter_sib(s):
+    def scatter_sib(s, which):
+        if which == 0:
+            @pl.when(s > 0)
+            def _():
+                pl.semaphore_wait(free_sib, 1)
+
+        sib_copies()[which].start()
+
+    def scatter_near(s, which):
         @pl.when(s > 0)
         def _():
-            pl.semaphore_wait(free_sib, 1)
-
-        for copy in sib_copies():
+            for copy in near_copies(which):
+                copy.wait_send()
+
+        sib_copies()[which].wait_recv()
+        top, bot = pl.ds(0, HD), pl.ds(HD, HD)
+        if which < 2:
+            m = which
+            fing[m] = owng[m, chip] + recg[m, chip].astype(f32)
+            sdg[m] = (owng[m, chip_d] + recg[m, chip_d].astype(f32)).astype(bf16)
+            far_x = owng[m, chip_x] + recg[m, chip_x].astype(f32)
+            far_y = owng[m, chip_y] + recg[m, chip_y].astype(f32)
+            if m == 0:
+                sxg[0] = far_x.astype(bf16)
+                owng[0, chip_y] = far_y
+            else:
+                syg[1] = far_y.astype(bf16)
+                owng[1, chip_x] = far_x
+
+            @pl.when(s > 0)
+            def _():
+                pl.semaphore_wait(free_diag.at[m], 1)
+                pl.semaphore_wait(free_block.at[m], 1)
+        else:
+            find[...] = ownd[chip] + recd[chip].astype(f32)
+            sdd[...] = (ownd[chip_d] + recd[chip_d].astype(f32)).astype(bf16)
+            sxd[top] = (ownd[chip_x, top] + recd[chip_x, top].astype(f32)).astype(bf16)
+            ownd[chip_x, bot] = ownd[chip_x, bot] + recd[chip_x, bot].astype(f32)
+            syd[bot] = (ownd[chip_y, bot] + recd[chip_y, bot].astype(f32)).astype(bf16)
+            ownd[chip_y, top] = ownd[chip_y, top] + recd[chip_y, top].astype(f32)
+
+            @pl.when(s < STEPS - 1)
+            def _():
+                signal(free_sib, sib)
+
+        for copy in near_copies(which):
             copy.start()
 
-    def scatter_diag(s):
+    def scatter_sum(s):
         @pl.when(s > 0)
         def _():
-            for copy in diag_copies():
+            for copy in sum_copies():
                 copy.wait_send()
 
-        for copy in sib_copies():
-            copy.wait_recv()
-        for m in range(2):
-            fing[m] = owng[m, chip] + recg[m, chip].astype(f32)
-            owng[m, chip_x] = owng[m, chip_x] + recg[m, chip_x].astype(f32)
-            owng[m, chip_y] = owng[m, chip_y] + recg[m, chip_y].astype(f32)
-            sdg[m] = (owng[m, chip_d] + recg[m, chip_d].astype(f32)).astype(bf16)
-        find[...] = ownd[chip] + recd[chip].astype(f32)
-        ownd[chip_x] = ownd[chip_x] + recd[chip_x].astype(f32)
-        ownd[chip_y] = ownd[chip_y] + recd[chip_y].astype(f32)
-        sdd[...] = (ownd[chip_d] + recd[chip_d].astype(f32)).astype(bf16)
-
-        @pl.when(s < STEPS - 1)
-        def _():
-            signal(free_sib, sib)
-
-        @pl.when(s > 0)
-        def _():
-            for sem in (free_diag.at[0], free_diag.at[1]):
-                pl.semaphore_wait(sem, 1)
-
-        for copy in diag_copies():
-            copy.start()
-
-    def scatter_block(s):
-        @pl.when(s > 0)
-        def _():
-            for copy in block_copies():
-                copy.wait_send()
-
-        for copy in diag_copies():
-            copy.wait_recv()
+        diag_arrived()
         top, bot = pl.ds(0, HD), pl.ds(HD, HD)
-        sxg[0] = owng[0, chip_x].astype(bf16)
         sxg[1] = (owng[1, chip_x] + rdg[1].astype(f32)).astype(bf16)
-        sxd[top] = ownd[chip_x, top].astype(bf16)
+        syg[0] = (owng[0, chip_y] + rdg[0].astype(f32)).astype(bf16)
         sxd[bot] = (ownd[chip_x, bot] + rdd[bot].astype(f32)).astype(bf16)
-        syg[0] = (owng[0, chip_y] + rdg[0].astype(f32)).astype(bf16)
-        syg[1] = owng[1, chip_y].astype(bf16)
         syd[top] = (ownd[chip_y, top] + rdd[top].astype(f32)).astype(bf16)
-        syd[bot] = ownd[chip_y, bot].astype(bf16)
 
         @pl.when(s < STEPS - 1)
         def _():
             signal(free_diag.at[0], xn)
             signal(free_diag.at[1], yn)
 
-        @pl.when(s > 0)
-        def _():
-            for sem in (free_block.at[0], free_block.at[1]):
-                pl.semaphore_wait(sem, 1)
-
-        for copy in block_copies():
+        for copy in sum_copies():
             copy.start()
 
     def scatter_final(s):
@@ -282,8 +324,7 @@
         def _():
             out_stored()
 
-        for copy in block_copies():
-            copy.wait_recv()
+        blocks_arrived()
         for m in range(2):
             og[m] = (fing[m] + bxg[m].astype(f32) + byg[m].astype(f32)).astype(bf16)
         od[...] = (find[...] + bxd[...].astype(f32) + byd[...].astype(f32)).T.astype(bf16)
@@ -301,12 +342,18 @@
     def tokens(t, n):
         return pl.ds(pl.multiple_of(t * n, n), n)
 
+    def store_at(rows, v):
+        vt = v.T
+        for d in range(N):
+            at[(d % 2 + k) % 2, d // 2, :, rows] = vt[d * RB : (d + 1) * RB]
+
+    def set_at(rows, wide):
+        store_at(rows, (wide * scale_of(wide)).astype(bf16))
+
     def set_a(rows, wide):
         v = (wide * scale_of(wide)).astype(bf16)
         a[rows, :] = v
-        vt = v.T
-        for d in range(N):
-            at[(d % 2 + k) % 2, d // 2, :, rows] = vt[d * RB : (d + 1) * RB]
+        store_at(rows, v)
 
     def store_saved(c, t):
         return pltpu.make_async_copy(saved.at[t % 2], saved_hbm.at[c, t], saved_sem.at[t % 2])
@@ -347,7 +394,8 @@
         set_a(rows, h[rows, :].astype(f32))
         dyt[:, rows] = dy[rows, :].T
 
-    gather_forward(0)
+    gather_forward_gu(0)
+    gather_forward_dn(0)
     gather_own_gu(1)
     gather_last(0)
     gather_done(0)
@@ -384,6 +432,12 @@
                 gather_own_dn(c + 2)
                 gather_forward(c + 1)
                 gather_own_gu(c + 2)
+                load_pieces(c + 1, (c + 1) % 2, (xn, yn), own=True)
+
+            @pl.when(t == TILES - 2)
+            def _():
+                gather_sib(c + 1, range(3))
+                load_pieces(c + 1, (c + 1) % 2, [2 * q + (1 - k) for q in (chip, chip_x, chip_y)])
 
         pltpu.make_async_copy(z, z_hbm.at[c], z_sem).start()
 
@@ -393,8 +447,9 @@
             acc[:, rows] += dot_nt(wd[slot], z[rows, :])
 
         gather_last(c + 1)
-        gather_done(c + 1)
-        load_weights(c + 1, (c + 1) % 2)
+        load_pieces(c + 1, (c + 1) % 2, (dn,))
+        gather_sib(c + 1, (3,))
+        load_pieces(c + 1, (c + 1) % 2, (2 * chip_d + (1 - k),))
 
     @pl.loop(0, T // VB)
     def _(t):
@@ -440,10 +495,17 @@
                         gather_forward(CH + 1)
                         gather_own_gu(CH + 2)
 
-                    @pl.when((t == 0) & (s == 1))
+                    @pl.when((t == 3) & (s == 0))
                     def _():
-                        gather_last(CH + 2)
-                        gather_forward(CH + 3)
+                        gather_last(CH + 1)
+
+                    @pl.when((t == 0) & (s > 0) & (s < 3))
+                    def _():
+                        gather_last(CH + 1 + s)
+
+                    @pl.when((t == 1) & (s > 0))
+                    def _():
+                        scatter_sum(s - 1)
 
             @pl.when(li > 0)
             def _():
@@ -460,9 +522,12 @@
                     def _():
                         load_saved(n + 2).start()
 
+                    @pl.when(t == 3)
+                    def _():
+                        scatter_sum(s - 1)
+
             @pl.when(s > 0)
             def _():
-                scatter_block(s - 1)
                 for copy in sib_copies():
                     copy.wait_send()
 
@@ -474,6 +539,14 @@
                     w = dot(at[...].reshape(D, T), grad[:, cols])
                     owng[m, :, :, cols] = w[:HD].reshape(4, RB, TB)
                     sibg[m, :, :, cols] = w[HD:].reshape(4, RB, TB).astype(bf16)
+
+                scatter_sib(s, m)
+                if m == 0:
+                    @pl.when(s > 0)
+                    def _():
+                        scatter_final(s - 1)
+
+            scatter_near(s, 0)
 
             @pl.when(li > 0)
             def _():
@@ -488,45 +561,47 @@
                     ownd[q] = jnp.where(k == 0, lo, hi)
                     sibd[q] = jnp.where(k == 0, hi, lo).astype(bf16)
 
-            scatter_sib(s)
+            scatter_sib(s, 2)
+            scatter_near(s, 1)
+
+            @pl.when(s == CH - 1)
+            def _():
+                pltpu.make_async_copy(x_hbm.at[0], a, in_sem.at[0]).start()
 
             @pl.when((s >= CH - 1) & (s < STEPS - 1))
             def _():
                 pltpu.make_async_copy(z_hbm.at[s - (CH - 1)], z, z_sem).start()
 
+            @pl.when(s < CH - 1)
+            def _():
+                gather_done(CH + 1 + s)
+
+            @pl.when(s < STEPS - 1)
+            def _():
+                load_weights((CH + s + 1) % STEPS, (c + 1) % 2)
+
             @pl.when(s == 0)
             def _():
-                gather_last(CH + 1)
-                gather_done(CH + 1)
                 gather_own_dn(CH + 3)
                 gather_forward(CH + 2)
                 gather_own_gu(CH + 3)
 
             @pl.when(s == 1)
             def _():
-                gather_done(CH + 2)
-                gather_last(CH + 3)
-
-            @pl.when(s == 2)
-            def _():
-                gather_done(CH + 3)
-
-            @pl.when(s < STEPS - 1)
-            def _():
-                load_weights((CH + s + 1) % STEPS, (c + 1) % 2)
+                gather_forward(CH + 3)
 
             @pl.loop(0, T // TB)
             def _(t):
                 rows = tokens(t, TB)
                 acc[:, rows] += dot_nt(wg[slot], dg[rows, :]) + dot_nt(wu[slot], du[rows, :])
 
-                @pl.when((t == 2) & (s > 0))
+                @pl.when(t == 1)
                 def _():
-                    scatter_final(s - 1)
-
-                @pl.when(t == 2)
-                def _():
-                    scatter_diag(s)
+                    scatter_near(s, 2)
+
+        @pl.when(li == 0)
+        def _():
+            pltpu.make_async_copy(x_hbm.at[0], a, in_sem.at[0]).wait()
 
         @pl.loop(0, T // VB)
         def _(t):
@@ -538,33 +613,30 @@
             dwide = (da * scale - wide * (along * scale * scale * scale)).astype(bf16)
             v = (dy[rows, :].astype(f32) + dwide.astype(f32)).astype(bf16)
             dy[rows, :] = v
-            dyt[:, rows] = v.T
-
-            @pl.when((li > 0) & (t == 3))
-            def _():
-                scatter_block(STEPS - 1)
-
-        @pl.when(li == 0)
-        def _():
-            again = pltpu.make_async_copy(x_hbm.at[0], h, in_sem.at[0])
-            again.start()
-            again.wait()
-
-            @pl.loop(0, T // VB)
-            def _(t):
-                rows = tokens(t, VB)
-                set_a(rows, h[rows, :].astype(f32))
-
-    store_dx = pltpu.make_async_copy(dy, dx_hbm.at[0], in_sem.at[1])
-    store_dx.start()
+
+            @pl.when(li == 0)
+            def _():
+                dyt[:, rows] = v.T
+                x = a[rows, :]
+                h[rows, :] = x
+                set_at(rows, x.astype(f32))
+
+            @pl.when(li > 0)
+            def _():
+                pltpu.make_async_copy(dy.at[rows], dx_hbm.at[0, rows], in_sem.at[1]).start()
+
+                @pl.when(t == 2)
+                def _():
+                    scatter_sum(STEPS - 1)
+
     last = STEPS - 1
     scatter_final(last)
-    for copy in sib_copies() + diag_copies() + block_copies():
+    for copy in (*sib_copies(), *near_copies(0), *near_copies(1), *near_copies(2), *sum_copies()):
         copy.wait_send()
     out_stored()
-    for copy in (*own_gu(last), *own_dn(last), *forward_copies(last), *last_copies(last)):
+    for copy in (*own_gu(last), *own_dn(last), *forward_gu(last), *forward_dn(last), *last_copies(last)):
         copy.wait_send()
-    store_dx.wait()
+    pltpu.make_async_copy(dy, dx_hbm.at[0], in_sem.at[1]).wait()
 
 
 def on_device(x, dy, w_gate, w_up, w_down):
@@ -592,7 +664,7 @@
         *[gu, down] * 6,
         pltpu.VMEM((2, RB, F), f32), pltpu.VMEM((D, CB), f32), gu, pltpu.VMEM((CB, D), bf16),
         pltpu.VMEM((2, 2, RB, F), bf16), pltpu.VMEM((STEPS, D, CB), bf16), pltpu.VMEM((2, 2, VB, F), f32),
-        dma((16,)), dma((STEPS, 16)), dma((2, 3)), dma((10,)), dma((10,)), dma((2,)), dma((4,)), dma((2,)), dma((2,)), dma,
+        dma((16,)), dma((STEPS, 16)), dma((2, 3)), dma((15,)), dma((15,)), dma((2,)), dma((4,)), dma((2,)), dma((2,)), dma,
         pltpu.SemaphoreType.REGULAR, pltpu.SemaphoreType.REGULAR((2,)), pltpu.SemaphoreType.REGULAR((2,)),
     ]
     return pl.pallas_call(

time: 357 us -> 356 us (level)
  no operation moved by 1% of the time
where the time goes in v3:
time: 356 us
  Pallas kernels  347 us (97%)
  local copies, waits for them, and re-layouts  8.2 us (2%)
    pallas_call x1, Pallas kernels, on_device(): pl.pallas_call(kernel, out_shape=shapes, in_specs=[hbm] * 5, out_specs=[h...  347 us
    unnamed x10, local copies, waits for them, and re-layouts  8.2 us

profile of v3, /device:TPU:0, one launch (start us, length us, event | category | flops | bytes accessed | tf_op | source)
XLA Modules:
  0.0 356.0 jit_solution(10013815303420104978)
XLA Ops:
  0.6 347.1 %layers.1 = (bf16[1,2048,640]{2,1,0:T(8,128)(2,1)}, bf16[2,80,4096]{2,1,0:T(8,128)(2,1)}, bf16[2,80,4096]{2,1,0:T(8,128)(2,1)}, bf16[2,512,640]{2,1,0:T(8,128)(2...) custom-call(bf16[1,2048,640]{2,1,0:T(8,128)(2,1)} %x_hbm.1, ...), custom_call_target="tpu_custom_call" | custom-call | tf_op jit(solution)/shard_map/layers/pallas_call | solution.py:670
  347.8 0.0 copy-start.2
  347.8 3.6 copy.13
  351.4 0.0 copy-done.2
  351.4 0.0 copy-start.1
  351.4 1.1 copy.14
  352.4 0.7 copy-done.1
  353.1 0.0 copy-start
  353.1 1.1 copy.15
  354.2 0.7 copy-done
  354.9 1.1 copy.16
Async XLA Ops:
  347.8 3.6 %copy-start.2 = (bf16[2,80,4096]{2,1,0:T(8,128)(2,1)S(1)}, bf16[2,80,4096]{2,1,0:T(8,128)(2,1)}, u32[]{:S(2)}) copy-start(bf16[2,80,4096]{2,1,0:T(8,128)(2,1)} %get-tuple-element.17) | copy-start | bytes 3932164
  351.4 1.8 copy-start.1
  353.1 1.8 copy-start

commit v4 on v3

--- a/solution.py
+++ b/solution.py
@@ -15,6 +15,8 @@
 STEPS = LAYERS * CH
 TB = 512
 VB = 256
+WB = 1024
+AB = 1024
 TILES = T // VB
 
 f32, bf16 = jnp.float32, jnp.bfloat16
@@ -397,6 +399,7 @@
     gather_forward_gu(0)
     gather_forward_dn(0)
     gather_own_gu(1)
+    gather_own_dn(2)
     gather_last(0)
     gather_done(0)
     load_weights(0, 0)
@@ -429,7 +432,6 @@
 
             @pl.when(t == 1)
             def _():
-                gather_own_dn(c + 2)
                 gather_forward(c + 1)
                 gather_own_gu(c + 2)
                 load_pieces(c + 1, (c + 1) % 2, (xn, yn), own=True)
@@ -441,12 +443,13 @@
 
         pltpu.make_async_copy(z, z_hbm.at[c], z_sem).start()
 
-        @pl.loop(0, T // TB)
+        @pl.loop(0, T // AB)
         def _(t):
-            rows = tokens(t, TB)
+            rows = tokens(t, AB)
             acc[:, rows] += dot_nt(wd[slot], z[rows, :])
 
         gather_last(c + 1)
+        gather_own_dn(c + 3)
         load_pieces(c + 1, (c + 1) % 2, (dn,))
         gather_sib(c + 1, (3,))
         load_pieces(c + 1, (c + 1) % 2, (2 * chip_d + (1 - k),))
@@ -459,12 +462,28 @@
         h[rows, :] = v
         set_a(rows, v.astype(f32))
 
+    gather_forward(CH + 1)
+    gather_own_gu(CH + 2)
+    gather_own_dn(CH + 3)
+
     pltpu.make_async_copy(z, z_hbm.at[CH - 1], z_sem).wait()
     for t in (0, 1):
         store_saved(CH - 1, t).wait()
     for t in (0, 1):
         load_saved(t).start()
 
+    def first_grads(c, t, slot):
+        rows = tokens(t, VB)
+        n = c * TILES + t
+        dz = dot(dy[rows, :], wd[slot]).astype(bf16).astype(f32)
+        load_saved(n).wait()
+        du[rows, :] = (dz * saved[n % 2, 0]).astype(bf16)
+        dg[rows, :] = (dz * saved[n % 2, 1]).astype(bf16)
+
+        @pl.when(n < CH * TILES - 2)
+        def _():
+            load_saved(n + 2).start()
+
     @pl.loop(0, LAYERS)
     def _(li):
         acc[...] = jnp.zeros_like(acc)
@@ -473,7 +492,14 @@
         def _(c):
             s = li * CH + c
             slot = c % 2
-            weights_loaded(slot)
+
+            @pl.when((li == 0) | (c == 0))
+            def _():
+                weights_loaded(slot)
+
+            @pl.when((li > 0) & (c < CH - 1))
+            def _():
+                load_weights(c + 1, (c + 1) % 2)
 
             @pl.when(li == 0)
             def _():
@@ -491,40 +517,30 @@
 
                     @pl.when((t == 0) & (s == 0))
                     def _():
-                        gather_own_dn(CH + 2)
-                        gather_forward(CH + 1)
-                        gather_own_gu(CH + 2)
+                        gather_last(CH + 1)
 
                     @pl.when((t == 3) & (s == 0))
                     def _():
-                        gather_last(CH + 1)
-
-                    @pl.when((t == 0) & (s > 0) & (s < 3))
+                        gather_forward(CH + 2)
+                        gather_own_gu(CH + 3)
+
+                    @pl.when((t == 3) & (s == 2))
                     def _():
-                        gather_last(CH + 1 + s)
-
-                    @pl.when((t == 1) & (s > 0))
+                        gather_last(CH + 3)
+
+                    @pl.when((t == 2) & (s > 0))
                     def _():
                         scatter_sum(s - 1)
 
-            @pl.when(li > 0)
+            @pl.when((li > 0) & (c == 0))
             def _():
                 @pl.loop(0, TILES)
                 def _(t):
-                    rows = tokens(t, VB)
-                    n = c * TILES + t
-                    dz = dot(dy[rows, :], wd[slot]).astype(bf16).astype(f32)
-                    load_saved(n).wait()
-                    du[rows, :] = (dz * saved[t % 2, 0]).astype(bf16)
-                    dg[rows, :] = (dz * saved[t % 2, 1]).astype(bf16)
-
-                    @pl.when(n < CH * TILES - 2)
-                    def _():
-                        load_saved(n + 2).start()
-
-                    @pl.when(t == 3)
-                    def _():
-                        scatter_sum(s - 1)
+                    first_grads(0, t, 0)
+
+            @pl.when(li > 0)
+            def _():
+                scatter_sum(s - 1)
 
             @pl.when(s > 0)
             def _():
@@ -533,18 +549,18 @@
 
             for m, grad in enumerate((dg, du)):
 
-                @pl.loop(0, F // TB)
+                @pl.loop(0, F // WB)
                 def _(n):
-                    cols = tokens(n, TB)
+                    cols = tokens(n, WB)
                     w = dot(at[...].reshape(D, T), grad[:, cols])
-                    owng[m, :, :, cols] = w[:HD].reshape(4, RB, TB)
-                    sibg[m, :, :, cols] = w[HD:].reshape(4, RB, TB).astype(bf16)
+                    owng[m, :, :, cols] = w[:HD].reshape(4, RB, WB)
+                    sibg[m, :, :, cols] = w[HD:].reshape(4, RB, WB).astype(bf16)
 
                 scatter_sib(s, m)
-                if m == 0:
-                    @pl.when(s > 0)
-                    def _():
-                        scatter_final(s - 1)
+
+            @pl.when(s > 0)
+            def _():
+                scatter_final(s - 1)
 
             scatter_near(s, 0)
 
@@ -552,12 +568,12 @@
             def _():
                 pltpu.make_async_copy(z_hbm.at[c], z, z_sem).wait()
 
-            @pl.loop(0, F // TB)
+            @pl.loop(0, F // WB)
             def _(n):
-                w = dot(dyt[...], z[:, tokens(n, TB)])
-                for i in range(TB // (2 * CB)):
+                w = dot(dyt[...], z[:, tokens(n, WB)])
+                for i in range(WB // (2 * CB)):
                     lo, hi = w[:, 2 * CB * i : 2 * CB * i + CB], w[:, 2 * CB * i + CB : 2 * CB * (i + 1)]
-                    q = n * (TB // (2 * CB)) + i
+                    q = n * (WB // (2 * CB)) + i
                     ownd[q] = jnp.where(k == 0, lo, hi)
                     sibd[q] = jnp.where(k == 0, hi, lo).astype(bf16)
 
@@ -576,28 +592,35 @@
             def _():
                 gather_done(CH + 1 + s)
 
-            @pl.when(s < STEPS - 1)
+            @pl.when(li == 0)
             def _():
                 load_weights((CH + s + 1) % STEPS, (c + 1) % 2)
 
-            @pl.when(s == 0)
-            def _():
-                gather_own_dn(CH + 3)
-                gather_forward(CH + 2)
-                gather_own_gu(CH + 3)
+            @pl.when((li > 0) & (c < CH - 1))
+            def _():
+                weights_loaded((c + 1) % 2)
 
             @pl.when(s == 1)
             def _():
                 gather_forward(CH + 3)
 
-            @pl.loop(0, T // TB)
+            @pl.loop(0, T // AB)
             def _(t):
-                rows = tokens(t, TB)
+                rows = tokens(t, AB)
                 acc[:, rows] += dot_nt(wg[slot], dg[rows, :]) + dot_nt(wu[slot], du[rows, :])
 
-                @pl.when(t == 1)
+                @pl.when((li > 0) & (c < CH - 1))
+                def _():
+                    for i in range(AB // VB):
+                        first_grads(c + 1, t * (AB // VB) + i, (c + 1) % 2)
+
+                @pl.when(t == 0)
                 def _():
                     scatter_near(s, 2)
+
+                @pl.when((t == 0) & (s == 0))
+                def _():
+                    gather_last(CH + 2)
 
         @pl.when(li == 0)
         def _():

time: 356 us -> 340 us (0.955)
  Pallas kernels: 347 us -> 331 us
    pallas_call x1, Pallas kernels: 347 us -> 331 us  [on_device(): pl.pallas_call(kernel, out_shape=shapes, in_specs=[hbm] * 5, out_specs=[h...]
where the time goes in v4:
time: 340 us
  Pallas kernels  331 us (97%)
  local copies, waits for them, and re-layouts  8.2 us (2%)
    pallas_call x1, Pallas kernels, on_device(): pl.pallas_call(kernel, out_shape=shapes, in_specs=[hbm] * 5, out_specs=[h...  331 us
    unnamed x10, local copies, waits for them, and re-layouts  8.2 us

profile of v4, /device:TPU:0, one launch (start us, length us, event | category | flops | bytes accessed | tf_op | source)
XLA Modules:
  0.0 339.7 jit_solution(9470835138880506082)
XLA Ops:
  0.6 330.8 %layers.1 = (bf16[1,2048,640]{2,1,0:T(8,128)(2,1)}, bf16[2,80,4096]{2,1,0:T(8,128)(2,1)}, bf16[2,80,4096]{2,1,0:T(8,128)(2,1)}, bf16[2,512,640]{2,1,0:T(8,128)(2...) custom-call(bf16[1,2048,640]{2,1,0:T(8,128)(2,1)} %x_hbm.1, ...), custom_call_target="tpu_custom_call" | custom-call | tf_op jit(solution)/shard_map/layers/pallas_call | solution.py:693
  331.5 0.0 copy-start.2
  331.5 3.6 %copy.13 = bf16[1,2048,640]{2,1,0:T(8,128)(2,1)} copy(bf16[1,2048,640]{2,1,0:T(8,128)(2,1)} %get-tuple-element.16) | data formatting | bytes 5242880
  335.0 0.0 copy-done.2
  335.0 0.0 copy-start.1
  335.0 1.1 copy.14
  336.1 0.7 copy-done.1
  336.8 0.0 copy-start
  336.8 1.1 copy.15
  337.9 0.7 copy-done
  338.6 1.1 copy.16
Async XLA Ops:
  331.5 3.6 %copy-start.2 = (bf16[2,80,4096]{2,1,0:T(8,128)(2,1)S(1)}, bf16[2,80,4096]{2,1,0:T(8,128)(2,1)}, u32[]{:S(2)}) copy-start(bf16[2,80,4096]{2,1,0:T(8,128)(2,1)} %get-tuple-element.17) | copy-start | bytes 3932164
  335.0 1.8 copy-start.1
  336.8 1.8 copy-start

commit v5 on v4

--- a/solution.py
+++ b/solution.py
@@ -16,6 +16,7 @@
 TB = 512
 VB = 256
 WB = 1024
+PIECES = 4 + 3 * LAYERS
 AB = 1024
 TILES = T // VB
 
@@ -203,40 +204,38 @@
             far(sibd, recd, rs_send.at[2], rs_recv.at[2], sib),
         )
 
+    def halves(which):
+        if which == 2:
+            return lambda g, d: (d.at[pl.ds(0, HD)], d.at[pl.ds(HD, HD)])
+        return lambda g, d: (g.at[which, :, pl.ds(0, F // 2)], g.at[which, :, pl.ds(F // 2, F // 2)])
+
     def near_copies(which):
-        top, bot = pl.ds(0, HD), pl.ds(HD, HD)
-        if which == 0:
-            return (
-                far(sdg.at[0], rdg.at[0], rs_send.at[3], rs_recv.at[3], xn),
-                far(sxg.at[0], bxg.at[0], rs_send.at[4], rs_recv.at[4], xn),
-            )
-        if which == 1:
-            return (
-                far(sdg.at[1], rdg.at[1], rs_send.at[5], rs_recv.at[5], yn),
-                far(syg.at[1], byg.at[1], rs_send.at[6], rs_recv.at[6], yn),
-            )
+        of, i = halves(which), 3 + 4 * which
         return (
-            far(sdd.at[top], rdd.at[top], rs_send.at[7], rs_recv.at[7], xn),
-            far(sdd.at[bot], rdd.at[bot], rs_send.at[8], rs_recv.at[8], yn),
-            far(sxd.at[top], bxd.at[top], rs_send.at[9], rs_recv.at[9], xn),
-            far(syd.at[bot], byd.at[bot], rs_send.at[10], rs_recv.at[10], yn),
+            far(of(sdg, sdd)[0], of(rdg, rdd)[0], rs_send.at[i], rs_recv.at[i], xn),
+            far(of(sdg, sdd)[1], of(rdg, rdd)[1], rs_send.at[i + 1], rs_recv.at[i + 1], yn),
+            far(of(sxg, sxd)[0], of(bxg, bxd)[0], rs_send.at[i + 2], rs_recv.at[i + 2], xn),
+            far(of(syg, syd)[1], of(byg, byd)[1], rs_send.at[i + 3], rs_recv.at[i + 3], yn),
         )
 
     def sum_copies():
-        top, bot = pl.ds(0, HD), pl.ds(HD, HD)
-        return (
-            far(sxg.at[1], bxg.at[1], rs_send.at[11], rs_recv.at[11], xn),
-            far(syg.at[0], byg.at[0], rs_send.at[12], rs_recv.at[12], yn),
-            far(sxd.at[bot], bxd.at[bot], rs_send.at[13], rs_recv.at[13], xn),
-            far(syd.at[top], byd.at[top], rs_send.at[14], rs_recv.at[14], yn),
-        )
+        copies = []
+        for which in range(3):
+            of, i = halves(which), 15 + 2 * which
+            copies.append(far(of(sxg, sxd)[1], of(bxg, bxd)[1], rs_send.at[i], rs_recv.at[i], xn))
+            copies.append(far(of(syg, syd)[0], of(byg, byd)[0], rs_send.at[i + 1], rs_recv.at[i + 1], yn))
+        return copies
 
     def diag_arrived():
-        for copy in (near_copies(0)[0], near_copies(1)[0], *near_copies(2)[:2]):
-            copy.wait_recv()
+        for which in range(3):
+            for copy in near_copies(which)[:2]:
+                copy.wait_recv()
 
     def blocks_arrived():
-        for copy in (near_copies(0)[1], near_copies(1)[1], *near_copies(2)[2:], *sum_copies()):
+        for which in range(3):
+            for copy in near_copies(which)[2:]:
+                copy.wait_recv()
+        for copy in sum_copies():
             copy.wait_recv()
 
     def store_out(j):
@@ -272,17 +271,17 @@
             sdg[m] = (owng[m, chip_d] + recg[m, chip_d].astype(f32)).astype(bf16)
             far_x = owng[m, chip_x] + recg[m, chip_x].astype(f32)
             far_y = owng[m, chip_y] + recg[m, chip_y].astype(f32)
+            sxg[m, :, : F // 2] = far_x[:, : F // 2].astype(bf16)
+            owng[m, chip_x, :, F // 2 :] = far_x[:, F // 2 :]
+            syg[m, :, F // 2 :] = far_y[:, F // 2 :].astype(bf16)
+            owng[m, chip_y, :, : F // 2] = far_y[:, : F // 2]
+
             if m == 0:
-                sxg[0] = far_x.astype(bf16)
-                owng[0, chip_y] = far_y
-            else:
-                syg[1] = far_y.astype(bf16)
-                owng[1, chip_x] = far_x
-
-            @pl.when(s > 0)
-            def _():
-                pl.semaphore_wait(free_diag.at[m], 1)
-                pl.semaphore_wait(free_block.at[m], 1)
+                @pl.when(s > 0)
+                def _():
+                    for sem in (free_diag, free_block):
+                        for i in range(2):
+                            pl.semaphore_wait(sem.at[i], 1)
         else:
             find[...] = ownd[chip] + recd[chip].astype(f32)
             sdd[...] = (ownd[chip_d] + recd[chip_d].astype(f32)).astype(bf16)
@@ -306,8 +305,10 @@
 
         diag_arrived()
         top, bot = pl.ds(0, HD), pl.ds(HD, HD)
-        sxg[1] = (owng[1, chip_x] + rdg[1].astype(f32)).astype(bf16)
-        syg[0] = (owng[0, chip_y] + rdg[0].astype(f32)).astype(bf16)
+        lo, hi = pl.ds(0, F // 2), pl.ds(F // 2, F // 2)
+        for m in range(2):
+            sxg[m, :, hi] = (owng[m, chip_x, :, hi] + rdg[m, :, hi].astype(f32)).astype(bf16)
+            syg[m, :, lo] = (owng[m, chip_y, :, lo] + rdg[m, :, lo].astype(f32)).astype(bf16)
         sxd[bot] = (ownd[chip_x, bot] + rdd[bot].astype(f32)).astype(bf16)
         syd[top] = (ownd[chip_y, top] + rdd[top].astype(f32)).astype(bf16)
 
@@ -451,8 +452,11 @@
         gather_last(c + 1)
         gather_own_dn(c + 3)
         load_pieces(c + 1, (c + 1) % 2, (dn,))
-        gather_sib(c + 1, (3,))
-        load_pieces(c + 1, (c + 1) % 2, (2 * chip_d + (1 - k),))
+
+        @pl.when(c < CH - 1)
+        def _():
+            gather_sib(c + 1, (3,))
+            load_pieces(c + 1, (c + 1) % 2, (2 * chip_d + (1 - k),))
 
     @pl.loop(0, T // VB)
     def _(t):
@@ -461,6 +465,11 @@
         v = (h[rows, :].astype(f32) + y.astype(f32)).astype(bf16)
         h[rows, :] = v
         set_a(rows, v.astype(f32))
+
+        @pl.when(t == 4)
+        def _():
+            gather_sib(CH, (3,))
+            load_pieces(CH, 0, (2 * chip_d + (1 - k),))
 
     gather_forward(CH + 1)
     gather_own_gu(CH + 2)
@@ -660,6 +669,29 @@
     for copy in (*own_gu(last), *own_dn(last), *forward_gu(last), *forward_dn(last), *last_copies(last)):
         copy.wait_send()
     pltpu.make_async_copy(dy, dx_hbm.at[0], in_sem.at[1]).wait()
+
+
+def pieces(refs):
+    for ref in refs:
+        if ref.shape[0] == 1:
+            for i in range(4):
+                yield ref.at[0, pl.ds(i * (T // 4), T // 4)]
+        else:
+            for i in range(LAYERS):
+                yield ref.at[i]
+
+
+def results(*refs):
+    here, there, held = refs[:4], refs[4:8], refs[8:12]
+    get, put = refs[12:]
+    trips = list(zip(pieces(here), pieces(held), pieces(there), strict=True))
+    for i, (src, mid, _) in enumerate(trips):
+        pltpu.make_async_copy(src, mid, get.at[i]).start()
+    for i, (src, mid, dst) in enumerate(trips):
+        pltpu.make_async_copy(src, mid, get.at[i]).wait()
+        pltpu.make_async_copy(mid, dst, put.at[i]).start()
+    for i, (_, mid, dst) in enumerate(trips):
+        pltpu.make_async_copy(mid, dst, put.at[i]).wait()
 
 
 def on_device(x, dy, w_gate, w_up, w_down):
@@ -687,10 +719,10 @@
         *[gu, down] * 6,
         pltpu.VMEM((2, RB, F), f32), pltpu.VMEM((D, CB), f32), gu, pltpu.VMEM((CB, D), bf16),
         pltpu.VMEM((2, 2, RB, F), bf16), pltpu.VMEM((STEPS, D, CB), bf16), pltpu.VMEM((2, 2, VB, F), f32),
-        dma((16,)), dma((STEPS, 16)), dma((2, 3)), dma((15,)), dma((15,)), dma((2,)), dma((4,)), dma((2,)), dma((2,)), dma,
+        dma((16,)), dma((STEPS, 16)), dma((2, 3)), dma((21,)), dma((21,)), dma((2,)), dma((4,)), dma((2,)), dma((2,)), dma,
         pltpu.SemaphoreType.REGULAR, pltpu.SemaphoreType.REGULAR((2,)), pltpu.SemaphoreType.REGULAR((2,)),
     ]
-    return pl.pallas_call(
+    grads = pl.pallas_call(
         kernel,
         out_shape=shapes,
         in_specs=[hbm] * 5,
@@ -699,6 +731,15 @@
         compiler_params=pltpu.CompilerParams(collective_id=0, has_side_effects=True, vmem_limit_bytes=67_000_000),
         name="layers",
     )(x, dy, w_gate, w_up, w_down)[:4]
+    return pl.pallas_call(
+        results,
+        out_shape=shapes[:4],
+        in_specs=[hbm] * 4,
+        out_specs=[hbm] * 4,
+        scratch_shapes=[pltpu.VMEM(s.shape, bf16) for s in shapes[:4]] + [dma((PIECES,)), dma((PIECES,))],
+        compiler_params=pltpu.CompilerParams(vmem_limit_bytes=67_000_000),
+        name="results",
+    )(*grads)
 
 
 def solution(mesh):

time: 340 us -> 336 us (0.988)
  local copies, waits for them, and re-layouts: 8.2 us -> 0 us
  Pallas kernels: 331 us -> 335 us
    unnamed x10 -> x0, local copies, waits for them, and re-layouts: 8.2 us -> none
    pallas_call x0 -> x1, Pallas kernels: none -> 5.53 us  [on_device(): pl.pallas_call(results, out_shape=shapes[:4], in_specs=[hbm] * 4, out_spe...]
where the time goes in v5:
time: 336 us; the launch traced here: 335 us
  Pallas kernels  335 us (100%)
    pallas_call x1, Pallas kernels, on_device(): pl.pallas_call(kernel, out_shape=shapes, in_specs=[hbm] * 5, out_specs=[h...  329 us

profile of v5, /device:TPU:0, one launch (start us, length us, event | category | flops | bytes accessed | tf_op | source)
XLA Modules:
  0.0 335.4 jit_solution(585826832351426382)
XLA Ops:
  0.6 329.1 %layers.1 = (bf16[1,2048,640]{2,1,0:T(8,128)(2,1)}, bf16[2,80,4096]{2,1,0:T(8,128)(2,1)}, bf16[2,80,4096]{2,1,0:T(8,128)(2,1)}, bf16[2,512,640]{2,1,0:T(8,128)(2...) custom-call(bf16[1,2048,640]{2,1,0:T(8,128)(2,1)} %x_hbm.1, ...), custom_call_target="tpu_custom_call" | custom-call | tf_op jit(solution)/shard_map/layers/pallas_call | solution.py:725
  329.7 5.5 %results.1 = (bf16[1,2048,640]{2,1,0:T(8,128)(2,1)}, bf16[2,80,4096]{2,1,0:T(8,128)(2,1)}, bf16[2,80,4096]{2,1,0:T(8,128)(2,1)}, bf16[2,512,640]{2,1,0:T(8,128)(2,1)}) custom-call(bf16[1,2048,640]{2,1,0:T(8,128)(2,1)} %get-tuple-element.8.refs_0_, bf16[2,80,4096]{2,1,0:T(8,128)(2,1)} %get-tuple-element.9.refs_1_, ...), custom_call_target="tpu_custom_call" | custom-call | tf_op jit(solution)/shard_map/results/pallas_call | solution.py:734

commit v6 on v5

--- a/solution.py
+++ b/solution.py
@@ -635,9 +635,9 @@
         def _():
             pltpu.make_async_copy(x_hbm.at[0], a, in_sem.at[0]).wait()
 
-        @pl.loop(0, T // VB)
+        @pl.loop(0, T // TB)
         def _(t):
-            rows = tokens(t, VB)
+            rows = tokens(t, TB)
             da = acc[:, rows].T.astype(bf16).astype(f32)
             wide = h[rows, :].astype(f32)
             scale = scale_of(wide)
@@ -657,7 +657,7 @@
             def _():
                 pltpu.make_async_copy(dy.at[rows], dx_hbm.at[0, rows], in_sem.at[1]).start()
 
-                @pl.when(t == 2)
+                @pl.when(t == 1)
                 def _():
                     scatter_sum(STEPS - 1)
 

time: 336 us -> 336 us (level)
  no operation moved by 1% of the time
where the time goes in v6:
time: 336 us; the launch traced here: 335 us
  Pallas kernels  334 us (99%)
    pallas_call x1, Pallas kernels, on_device(): pl.pallas_call(kernel, out_shape=shapes, in_specs=[hbm] * 5, out_specs=[h...  329 us

profile of v6, /device:TPU:0, one launch (start us, length us, event | category | flops | bytes accessed | tf_op | source)
XLA Modules:
  0.0 335.2 jit_solution(5178585690977364779)
XLA Ops:
  0.6 328.9 %layers.1 = (bf16[1,2048,640]{2,1,0:T(8,128)(2,1)}, bf16[2,80,4096]{2,1,0:T(8,128)(2,1)}, bf16[2,80,4096]{2,1,0:T(8,128)(2,1)}, bf16[2,512,640]{2,1,0:T(8,128)(2...) custom-call(bf16[1,2048,640]{2,1,0:T(8,128)(2,1)} %x_hbm.1, ...), custom_call_target="tpu_custom_call" | custom-call | tf_op jit(solution)/shard_map/layers/pallas_call | solution.py:725
  329.5 5.5 %results.1 = (bf16[1,2048,640]{2,1,0:T(8,128)(2,1)}, bf16[2,80,4096]{2,1,0:T(8,128)(2,1)}, bf16[2,80,4096]{2,1,0:T(8,128)(2,1)}, bf16[2,512,640]{2,1,0:T(8,128)(2,1)}) custom-call(bf16[1,2048,640]{2,1,0:T(8,128)(2,1)} %get-tuple-element.8.refs_0_, bf16[2,80,4096]{2,1,0:T(8,128)(2,1)} %get-tuple-element.9.refs_1_, ...), custom_call_target="tpu_custom_call" | custom-call | tf_op jit(solution)/shard_map/results/pallas_call | solution.py:734
